TPU v7x, 16 devices: a whole 2x2x2 slice. The times are simulated.
16 devices in a mesh: cp: 16 (over z, y, x, core).
Axes of the slice: x: 2, y: 2, z: 2, core: 2. Of those that a mesh axis runs over, the one named last changes fastest.
Arguments:
- queries: bfloat16 [4096, 16, 192], P('cp')
- latent: bfloat16 [4096, 512], P('cp')
- key_rope: bfloat16 [4096, 64], P('cp')
- w_uk: bfloat16 [512, 16, 128], replicated
- w_uv: bfloat16 [512, 16, 128], replicated
- d_out: bfloat16 [4096, 16, 128], P('cp')
Outputs:
- output 1: bfloat16 [4096, 16, 128], P('cp')
- output 2: bfloat16 [4096, 16, 192], P('cp')
- output 3: bfloat16 [4096, 512], P('cp')
- output 4: bfloat16 [4096, 64], P('cp')
- output 5: float32 [512, 16, 128], replicated
- output 6: float32 [512, 16, 128], replicated
All inputs are finite; a program needn't handle non-finite values.
Results may differ from a plain program's by a relative error of at most 0.016657.
Values are sent between devices in bfloat16 or wider.
A program may use at most 1 GiB of HBM per device.

v0:
```python
import math
import jax
import jax.numpy as jnp
from jax import lax
from jax.sharding import PartitionSpec as P


def solution(mesh):
    n_dev = mesh.shape["cp"]
    seq_spec = P("cp")

    def gather_all(k_nope, values, key_rope):
        k_all = lax.all_gather(k_nope, "cp", tiled=True)
        v_all = lax.all_gather(values, "cp", tiled=True)
        r_all = lax.all_gather(key_rope, "cp", tiled=True)
        return k_all, v_all, r_all

    def local_step(queries, latent, key_rope, w_uk, w_uv, d_out):
        tok_count = queries.shape[0]
        nope_dim = w_uk.shape[-1]
        score_scale = 1.0 / math.sqrt(queries.shape[-1])
        dev_index = lax.axis_index("cp")
        q_nope = queries[:, :, :nope_dim]
        q_rope = queries[:, :, nope_dim:]
        q_pos = dev_index * tok_count + jnp.arange(tok_count)
        visible = jnp.arange(tok_count * n_dev)[None, :] <= q_pos[:, None]

        def masked_scores(k_all, r_all):
            scores = (jnp.einsum("qhd,khd->hqk", q_nope, k_all, preferred_element_type=jnp.float32)
                      + jnp.einsum("qhd,kd->hqk", q_rope, r_all, preferred_element_type=jnp.float32)) * score_scale
            return jnp.where(visible[None], scores, -1e30)

        k_nope = jnp.einsum("tl,lhd->thd", latent, w_uk, preferred_element_type=jnp.float32).astype(jnp.bfloat16)
        values = jnp.einsum("tl,lhd->thd", latent, w_uv, preferred_element_type=jnp.float32).astype(jnp.bfloat16)

        k_all, v_all, r_all = gather_all(k_nope, values, key_rope)
        scores = masked_scores(k_all, r_all)
        row_max = jnp.max(scores, axis=-1, keepdims=True)
        exp_scores = jnp.exp(scores - row_max)
        row_sum = jnp.sum(exp_scores, axis=-1, keepdims=True)
        log_norm = row_max + jnp.log(row_sum)
        fwd_prob = (exp_scores / row_sum).astype(jnp.bfloat16)
        attn_out = jnp.einsum("hqk,khd->qhd", fwd_prob, v_all, preferred_element_type=jnp.float32).astype(jnp.bfloat16)

        k_all, v_all, r_all = gather_all(k_nope, values, key_rope)
        attn_prob = jnp.exp(masked_scores(k_all, r_all) - log_norm)
        prob_b = attn_prob.astype(jnp.bfloat16)
        d_prob = jnp.einsum("qhd,khd->hqk", d_out, v_all, preferred_element_type=jnp.float32)
        row_delta = jnp.einsum("qhd,qhd->hq", d_out, attn_out, preferred_element_type=jnp.float32)[:, :, None]
        d_score = (attn_prob * (d_prob - row_delta) * score_scale).astype(jnp.bfloat16)
        d_q_nope = jnp.einsum("hqk,khd->qhd", d_score, k_all, preferred_element_type=jnp.float32)
        d_q_rope = jnp.einsum("hqk,kd->qhd", d_score, r_all, preferred_element_type=jnp.float32)
        d_query = jnp.concatenate([d_q_nope, d_q_rope], axis=-1).astype(jnp.bfloat16)
        dk_part = jnp.einsum("hqk,qhd->khd", d_score, q_nope, preferred_element_type=jnp.float32).astype(jnp.bfloat16)
        dv_part = jnp.einsum("hqk,qhd->khd", prob_b, d_out, preferred_element_type=jnp.float32).astype(jnp.bfloat16)
        dr_part = jnp.einsum("hqk,qhd->kd", d_score, q_rope, preferred_element_type=jnp.float32).astype(jnp.bfloat16)
        d_k_nope = lax.psum_scatter(dk_part, "cp", scatter_dimension=0, tiled=True)
        d_values = lax.psum_scatter(dv_part, "cp", scatter_dimension=0, tiled=True)
        d_key_rope = lax.psum_scatter(dr_part, "cp", scatter_dimension=0, tiled=True)
        d_latent = (jnp.einsum("thd,lhd->tl", d_k_nope, w_uk, preferred_element_type=jnp.float32)
                    + jnp.einsum("thd,lhd->tl", d_values, w_uv, preferred_element_type=jnp.float32)).astype(jnp.bfloat16)
        d_w_uk = lax.psum(jnp.einsum("tl,thd->lhd", latent, d_k_nope, preferred_element_type=jnp.float32), "cp")
        d_w_uv = lax.psum(jnp.einsum("tl,thd->lhd", latent, d_values, preferred_element_type=jnp.float32), "cp")
        return attn_out, d_query, d_latent, d_key_rope, d_w_uk, d_w_uv

    return jax.shard_map(local_step, mesh=mesh,
                         in_specs=(seq_spec, seq_spec, seq_spec, P(), P(), seq_spec),
                         out_specs=(seq_spec, seq_spec, seq_spec, seq_spec, P(), P()),
                         check_vma=False)
```

profile of v0, /device:TPU:0, one launch (start us, length us, event | category | flops | bytes accessed | tf_op | source)
XLA Modules:
  0.0 822.9 jit_solution(5845376503044885702)
XLA Ops:
  7.2 3.5 fusion.24
  10.8 0.0 all-gather.3.cloned.1.call-start
  10.8 2.7 fusion.21
  13.6 21.1 %all_gather.14 = bf16[4096,64]{0,1:T(8,128)(2,1)} all-gather(bf16[256,64]{0,1:T(8,128)(2,1)} %param.8), channel_id=1, replica_groups=mesh['cp'=16] {'cp'}, dimensions={0}, use_global_device_ids=true | all-gather | bytes 557056 | tf_op jit(solution)/shard_map/all_gather | solution.py:15
  34.7 0.7 iota_compare_fusion
  35.4 58.5 %all-gather.5.cloned.1.call-done = bf16[4096,16,128]{2,0,1:T(8,128)(2,1)} async-done(((bf16[256,16,128]{2,0,1:T(8,128)(2,1)}), bf16[4096,16,128]{2,0,1:T(8,128)(2,1)}) %all-gather.5.cloned.1.call-update) | async-done | bytes 16777232 | tf_op jit(solution)/shard_map/all_gather | solution.py:13
  93.9 28.8 %fusion.44 = f32[16,4096,256]{2,1,0:T(8,128)} fusion(bf16[4096,16,128]{2,0,1:T(8,128)(2,1)} %all-gather.5.cloned.1.call-done, bf16[256,16,192]{0,2,1:T(8,128)(2,1)} %param.6), kind=kOutput, calls=%fused_computation.45 | convolution fusion | flops 4294967296 | bytes 84934656 | tf_op jit(solution)/shard_map/qhd,khd->hqk/dot_general | solution.py:29
  122.6 44.2 %fusion.55 = (f32[16,256]{1,0:T(8,128)S(1)}, f32[16,256,4096]{1,2,0:T(8,128)}) fusion(bf16[256,16,192]{0,2,1:T(8,128)(2,1)} %param.6, bf16[4096,64]{0,1:T(8,128)(2,1)} %all_gather.14, f32[16,4096,256]{2,1,0:T(8,128)} %fusion.44, pred[256,4096]{0,1:T(8,128)(4,1)S(1)} %iota_compare_fusion), kind=kOutput, calls=%fused_computation.58 | convolution fusion | flops 2214588416 | bytes 136331264 | tf_op jit(solution)/shard_map/qhd,kd->hqk/dot_general | solution.py:30
  166.8 21.0 %fusion.4 = f32[16,256]{1,0:T(8,128)S(1)} fusion(f32[16,256,4096]{1,2,0:T(8,128)} %get-tuple-element.15, f32[16,256]{1,0:T(8,128)S(1)} %get-tuple-element.14), kind=kLoop, calls=%fused_computation.9 | loop fusion | flops 33550336 | bytes 67141632 | tf_op jit(solution)/shard_map/reduce_sum | solution.py:40
  187.9 30.4 %bitcast_convert_fusion = (f32[16,256,128]{1,2,0:T(8,128)}, bf16[16,128,256]{2,1,0:T(8,128)(2,1)}) fusion(bf16[4096,16,128]{2,0,1:T(8,128)(2,1)} %all-gather.3.cloned.1.call-done, f32[16,256,4096]{1,2,0:T(8,128)} %get-tuple-element.15, f32[16,256]{1,0:T(8,128)S(1)} %fusion.4, f32[16,256]{1,0:T(8,128)S(1)} %get-tuple-element.14), kind=kOutput, calls=%fused_computation.42 | convolution fusion | flops 4346347520 | bytes 87064576 | tf_op jit(solution)/shard_map/hqk,khd->qhd/dot_general | solution.py:43
  218.4 3.0 copy.37
  221.4 2.2 multiply_reduce_fusion
  223.6 0.1 copy.38
  223.7 40.8 %fusion.1 = bf16[16,256,4096]{1,2,0:T(8,128)(2,1)} fusion(f32[16,256,4096]{1,2,0:T(8,128)} %get-tuple-element.15, bf16[4096,16,128]{2,0,1:T(8,128)(2,1)} %all-gather.3.cloned.1.call-done, f32[16,256]{1,0:T(8,128)S(1)} %copy.38, f32[16,256]{1,0:T(8,128)S(1)} %log_add_fusion, bf16[256,16,128]{2,1,0:T(8,128)(2,1)S(1)} %copy-done.1), kind=kOutput, calls=%fused_computation.2 | convolution fusion | flops 4378853376 | bytes 118521856 | tf_op jit(solution)/shard_map/qhd,khd->hqk/dot_general | solution.py:48
  264.5 21.2 %convert_bitcast_fusion.1 = bf16[4096,16,128]{2,0,1:T(8,128)(2,1)} fusion(bf16[16,256,4096]{1,2,0:T(8,128)(2,1)} %fusion.1, bf16[256,16,192]{0,2,1:T(8,128)(2,1)} %param.6), kind=kOutput, calls=%fused_computation.15 | convolution fusion | flops 4303355904 | bytes 51380224 | tf_op jit(solution)/shard_map/hqk,qhd->khd/dot_general | solution.py:54
  285.7 29.3 %convert_bitcast_fusion = bf16[4096,16,128]{2,0,1:T(8,128)(2,1)} fusion(f32[16,256,4096]{1,2,0:T(8,128)} %get-tuple-element.15, f32[16,256]{1,0:T(8,128)S(1)} %log_add_fusion, bf16[256,16,128]{2,1,0:T(8,128)(2,1)S(1)} %copy-done.1), kind=kOutput, calls=%fused_computation.14 | convolution fusion | flops 4336910336 | bytes 84951040 | tf_op jit(solution)/shard_map/hqk,qhd->khd/dot_general | solution.py:55
  315.1 148.0 %reduce-scatter.4.cloned.1.call-done = bf16[256,16,128]{2,0,1:T(8,128)(2,1)} async-done(((bf16[4096,16,128]{2,0,1:T(8,128)(2,1)}), bf16[256,16,128]{2,0,1:T(8,128)(2,1)}) %reduce-scatter.4.cloned.1.call-update) | async-done | bytes 1048592 | tf_op jit(solution)/shard_map/reduce_scatter | solution.py:57
  463.1 4.0 convolution_bitcast_fusion.2
  467.1 173.7 %reduce-scatter.6.cloned.1.call-done = bf16[256,16,128]{2,0,1:T(8,128)(2,1)} async-done(((bf16[4096,16,128]{2,0,1:T(8,128)(2,1)}), bf16[256,16,128]{2,0,1:T(8,128)(2,1)}) %reduce-scatter.6.cloned.1.call-update) | async-done | bytes 1048592 | tf_op jit(solution)/shard_map/reduce_scatter | solution.py:58
  640.8 4.0 convolution_bitcast_fusion.1
  644.8 0.3 reduce-scatter.8.cloned.1.call-start
  645.1 21.5 %fusion.12 = bf16[4096,64]{0,1:T(8,128)(2,1)} fusion(bf16[16,256,4096]{1,2,0:T(8,128)(2,1)} %fusion.1, bf16[256,16,192]{0,2,1:T(8,128)(2,1)} %param.6), kind=kOutput, calls=%fused_computation.17 | convolution fusion | flops 2147745792 | bytes 34603008 | tf_op jit(solution)/shard_map/hqk,qhd->kd/dot_general | solution.py:56
  666.7 18.0 %fusion.28 = bf16[256,16,128]{0,2,1:T(8,128)(2,1)S(1)} fusion(bf16[4096,16,128]{2,0,1:T(8,128)(2,1)} %all-gather.5.cloned.1.call-done, bf16[16,256,4096]{1,2,0:T(8,128)(2,1)} %fusion.1), kind=kOutput, calls=%fused_computation.35 | convolution fusion | flops 4295491584 | bytes 51380224 | tf_op jit(solution)/shard_map/hqk,khd->qhd/dot_general | solution.py:51
  684.6 14.4 %fusion.29 = bf16[256,16,64]{0,2,1:T(8,128)(2,1)} fusion(bf16[16,256,4096]{1,2,0:T(8,128)(2,1)} %fusion.1, bf16[4096,64]{0,1:T(8,128)(2,1)S(1)} %copy-done.2), kind=kOutput, calls=%fused_computation.37 | convolution fusion | flops 2147745792 | bytes 34603008 | tf_op jit(solution)/shard_map/hqk,kd->qhd/dot_general | solution.py:52
  699.0 2.6 copy.27
  701.7 2.3 pad_maximum_fusion
  704.0 2.0 fusion.30
  705.9 3.4 fusion.39
  709.3 50.3 %all-reduce.3.cloned.1.call-done = (f32[512,16,128]{0,2,1:T(8,128)}, f32[512,16,128]{0,2,1:T(8,128)}) async-done(((f32[512,16,128]{0,2,1:T(8,128)}, f32[512,16,128]{0,2,1:T(8,128)}), (f32[512,16,128]{0,2,1:T(8,128)}, f32[512,16,128]{0,2,1:T(8,128)})) %all-reduce.3.cloned.1.call-update) | async-done | bytes 8388624 | tf_op jit(solution)/shard_map/psum | solution.py:62
  759.6 5.4 copy.28
  765.0 5.4 copy.29
  770.5 45.6 %reduce-scatter.8.cloned.1.call-done = bf16[256,64]{0,1:T(8,128)(2,1)} async-done(((bf16[4096,64]{0,1:T(8,128)(2,1)}), bf16[256,64]{0,1:T(8,128)(2,1)}) %reduce-scatter.8.cloned.1.call-update) | async-done | bytes 32784 | tf_op jit(solution)/shard_map/reduce_scatter | solution.py:59
  (21 shorter events, 0.3 us)
Async XLA Ops:
  7.2 3.7 copy-start
  7.2 86.7 %all-gather.5.cloned.1.call-start = ((), (), s32[]{:S(2)}) async-start(), calls=%async_computation.4 | async-start | bytes 17825792 | tf_op jit(solution)/shard_map/all_gather | solution.py:13
  10.8 177.1 %all-gather.3.cloned.1.call-start = ((), (), s32[]{:S(2)}) async-start(), calls=%async_computation.3 | async-start | bytes 17825792 | tf_op jit(solution)/shard_map/all_gather | solution.py:14
  13.5 449.6 %reduce-scatter.4.cloned.1.call-start = ((), (), s32[]{:S(2)}) async-start(), calls=%async_computation.5 | async-start | bytes 17825792 | tf_op jit(solution)/shard_map/reduce_scatter | solution.py:57
  187.9 33.5 %copy-start.1 = (bf16[256,16,128]{2,1,0:T(8,128)(2,1)S(1)}, bf16[256,16,128]{2,1,0:T(8,128)(2,1)}, u32[]{:S(2)}) copy-start(bf16[256,16,128]{2,1,0:T(8,128)(2,1)} %param.11) | copy-start | bytes 3145732
  285.7 355.1 %reduce-scatter.6.cloned.1.call-start = ((), (), s32[]{:S(2)}) async-start(), calls=%async_computation.6 | async-start | bytes 17825792 | tf_op jit(solution)/shard_map/reduce_scatter | solution.py:58
  315.0 148.1 %copy-start.3 = (bf16[256,512]{1,0:T(8,128)(2,1)S(1)}, bf16[256,512]{1,0:T(8,128)(2,1)}, u32[]{:S(2)}) copy-start(bf16[256,512]{1,0:T(8,128)(2,1)} %param.7) | copy-start | bytes 786436
  315.0 444.6 %all-reduce.3.cloned.1.call-start = ((), (), s32[]{:S(2)}) async-start(), calls=%async_computation.8 | async-start | bytes 16777216 | tf_op jit(solution)/shard_map/psum | solution.py:62
  644.8 171.3 %reduce-scatter.8.cloned.1.call-start = ((), (), s32[]{:S(2)}) async-start(), calls=%async_computation.7 | async-start | bytes 557056 | tf_op jit(solution)/shard_map/reduce_scatter | solution.py:59
  666.6 18.0 %copy-start.2 = (bf16[4096,64]{0,1:T(8,128)(2,1)S(1)}, bf16[4096,64]{0,1:T(8,128)(2,1)}, u32[]{:S(2)}) copy-start(bf16[4096,64]{0,1:T(8,128)(2,1)} %all_gather.14) | copy-start | bytes 1572868
Sparse Core Ops, SparseCore 0:
  10.9 82.9 all-gather.4
  96.7 77.1 all-gather.2
  285.8 177.2 reduce-scatter.3
  465.2 175.4 reduce-scatter.5
  646.6 112.9 all-reduce.2
  762.3 53.7 reduce-scatter.7
where the time goes:
time: 824 us; the launch traced here: 823 us
  waiting for transfers between devices  476 us (58%)
  matrix products  268 us (33%)
  other arithmetic  26.2 us (3%)
  blocking collectives  21.1 us (3%)
  local copies, waits for them, and re-layouts  16.6 us (2%)
  between operations  14.2 us (2%)
    reduce_scatter x1, waiting for transfers between devices, local_step(): d_values = lax.psum_scatter(dv_part, 'cp', scatter_dimension=0, tiled=True)  174 us
    reduce_scatter x1, waiting for transfers between devices, local_step(): d_k_nope = lax.psum_scatter(dk_part, 'cp', scatter_dimension=0, tiled=True)  148 us
    all_gather x1, waiting for transfers between devices, gather_all(): k_all = lax.all_gather(k_nope, 'cp', tiled=True)  58.5 us
    psum x1, waiting for transfers between devices, local_step(): lax.psum(jnp.einsum('tl,thd->lhd', latent, d_k_nope, preferred_element_ty...  50.3 us
    reduce_scatter x1, waiting for transfers between devices, local_step(): lax.psum_scatter(dr_part, 'cp', scatter_dimension=0, tiled=True)  45.6 us
    dot_general x1, matrix products, masked_scores(): jnp.einsum('qhd,kd->hqk', q_rope, r_all, preferred_element_type=jnp.float32)  44.2 us
    dot_general x1, matrix products, local_step(): jnp.einsum('qhd,khd->hqk', d_out, v_all, preferred_element_type=jnp.float32)  40.8 us
    dot_general x1, matrix products, local_step(): jnp.einsum('hqk,khd->qhd', fwd_prob, v_all, preferred_element_type=jnp.fl...  30.4 us
  transfers between devices with their start and end apart: 6, of which 5 were waited for; matrix products, arithmetic and copies ran while one was open for 25% of the time, Pallas kernels for 0%

commit v1 on v0

v1 whole, which is shorter than its diff:
```python
import math
import jax
import jax.numpy as jnp
from jax import lax
from jax.experimental import pallas as pl
from jax.experimental.pallas import tpu as pltpu
from jax.sharding import PartitionSpec as P

MESH = pl.DeviceIdType.MESH
BF16 = jnp.bfloat16
F32 = jnp.float32

N = 16
T = 256
L = 512
D = 128
R = 64
QK = D + R
TK = 512
NT = 8
C_CHUNK = 96
W_CHUNK = 344
SCALE = 1.0 / math.sqrt(QK)
EXP_C = SCALE * math.log2(math.e)


def nt_dot(a, b):
    return lax.dot_general(a, b, (((1,), (1,)), ((), ())), preferred_element_type=F32)


def nn_dot(a, b):
    return lax.dot_general(a, b, (((1,), (0,)), ((), ())), preferred_element_type=F32)


def flip(x, bit):
    return x + bit * (1 - 2 * lax.rem(lax.div(x, bit), 2))


def xor(x, s):
    for bit in (1, 2, 4, 8):
        on = lax.rem(lax.div(s, bit), 2)
        x = x + on * bit * (1 - 2 * lax.rem(lax.div(x, bit), 2))
    return x


def fold(x, reduce):
    return reduce(x.reshape(x.shape[0] // 8, 8, x.shape[1]), axis=0)


def transpose(x):
    return jnp.transpose(x, (1, 0))


class Gather:
    def __init__(self, me, own, buf, chunk, send_sem, recv_sem, sib_send, sib_recv):
        self.me, self.own, self.buf, self.chunk = me, own, buf, chunk
        self.send_sem, self.recv_sem = send_sem, recv_sem
        self.sib_send, self.sib_recv = sib_send, sib_recv

    def axes(self, k):
        out = []
        for t in range(3):
            axis = lax.rem(k + t, 3)
            out.append(2 + axis * (axis + 1))
        return out

    def make(self, k, masks, mask, target, send_sem, recv_sem):
        src = self.me
        for bit in masks:
            src = flip(src, bit)
        rows = pl.ds(k * self.chunk, self.chunk)
        slot = k * 8 + lax.div(mask, 2)
        first = self.own.at[rows, :] if not masks else self.buf.at[src, rows, :]
        return pltpu.make_async_remote_copy(
            src_ref=first, dst_ref=self.buf.at[src, rows, :], send_sem=send_sem.at[slot], recv_sem=recv_sem.at[slot],
            device_id=(target,), device_id_type=MESH)

    def hop(self, k, masks, bit):
        return self.make(k, masks, sum(masks) + bit, flip(self.me, bit), self.send_sem, self.recv_sem)

    def sib(self, k, masks):
        return self.make(k, masks, sum(masks), flip(self.me, 1), self.sib_send, self.sib_recv)

    def arrived(self, k, masks):
        self.make(k, masks, sum(masks), flip(self.me, 1), self.send_sem, self.recv_sem).wait_recv()

    def stage0(self):
        for t in range(3):
            def send(k, carry):
                self.hop(k, (), self.axes(k)[t]).start()
                return carry
            lax.fori_loop(0, 3, send, 0)

        def send_sib(k, carry):
            self.sib(k, ()).start()
            return carry
        lax.fori_loop(0, 3, send_sib, 0)

    def stage1(self):
        def step(k, carry):
            a, b, c = self.axes(k)
            self.arrived(k, (a,))
            self.hop(k, (a,), b).start()
            self.hop(k, (a,), c).start()
            self.sib(k, (a,)).start()
            return carry
        lax.fori_loop(0, 3, step, 0)

    def stage2(self):
        for both in (False, True):
            def step(k, carry):
                a, b, c = self.axes(k)
                masks = (a, b) if both else (b,)
                self.arrived(k, masks)
                self.hop(k, masks, c).start()
                self.sib(k, masks).start()
                return carry
            lax.fori_loop(0, 3, step, 0)

    def stage3(self):
        for extra in range(4):
            def step(k, carry):
                a, b, c = self.axes(k)
                masks = ((c,), (a, c), (b, c), (a, b, c))[extra]
                self.arrived(k, masks)
                self.sib(k, masks).start()
                return carry
            lax.fori_loop(0, 3, step, 0)

    def finish(self):
        sibling = flip(self.me, 1)

        def step(n, carry):
            k, half = lax.div(n, 8), lax.rem(n, 8)
            rows = pl.ds(k * self.chunk, self.chunk)
            ref = self.buf.at[xor(sibling, 2 * half), rows, :]
            pltpu.make_async_remote_copy(
                src_ref=ref, dst_ref=ref, send_sem=self.sib_send.at[n], recv_sem=self.sib_recv.at[n],
                device_id=(sibling,), device_id_type=MESH).wait_recv()
            return carry
        lax.fori_loop(0, 24, step, 0)

    def drain(self):
        def step(n, carry):
            k, half = lax.div(n, 8), lax.rem(n, 8)
            rows = pl.ds(k * self.chunk, self.chunk)
            ref = self.buf.at[xor(self.me, 2 * half), rows, :]
            pltpu.make_async_remote_copy(
                src_ref=ref, dst_ref=ref, send_sem=self.sib_send.at[n], recv_sem=self.sib_recv.at[n],
                device_id=(flip(self.me, 1),), device_id_type=MESH).wait_send()

            @pl.when(half > 0)
            def _():
                pltpu.make_async_remote_copy(
                    src_ref=ref, dst_ref=ref, send_sem=self.send_sem.at[n], recv_sem=self.recv_sem.at[n],
                    device_id=(flip(self.me, 1),), device_id_type=MESH).wait_send()
            return carry
        lax.fori_loop(0, 24, step, 0)


def kernel(qt_ref, do_ref, c_ref, rt_ref, wuk_ref, wuv_ref,
           o_ref, dq_ref, dc_ref, drt_ref, dw_ref,
           in_q, in_do, stage_o, stage_dq, stage_g, in_g, call, kcat, kt, v, vt, sbuf, qz, dk, dv, ot, dqt, wuk, wuv, dw_own,
           q_send, q_recv, do_send, do_recv, o_send, o_recv, dq_send, dq_recv, g_send, g_recv, local_sem,
           c_send, c_recv, cs_send, cs_recv, w_send, w_recv, ws_send, ws_recv):
    me = lax.axis_index("cp")

    loads = [
        pltpu.make_async_copy(wuk_ref, wuk, local_sem.at[0]),
        pltpu.make_async_copy(wuv_ref, wuv, local_sem.at[1]),
        pltpu.make_async_copy(c_ref, call.at[me, pl.ds(0, T), :], local_sem.at[2]),
        pltpu.make_async_copy(rt_ref.at[pl.ds(0, 32), :], call.at[me, pl.ds(T, 32), pl.ds(0, T)], local_sem.at[3]),
        pltpu.make_async_copy(rt_ref.at[pl.ds(32, 32), :], call.at[me, pl.ds(T, 32), pl.ds(T, T)], local_sem.at[4]),
    ]
    for load in loads[::-1]:
        load.start()

    barrier = pltpu.get_barrier_semaphore()

    def hello(s, carry):
        pl.semaphore_signal(barrier, inc=1, device_id=(xor(me, s),), device_id_type=MESH)
        return carry

    lax.fori_loop(1, N, hello, 0)
    for load in loads[2:]:
        load.wait()
    pl.semaphore_wait(barrier, N - 1)

    def send(src, dst, s, send_sem, recv_sem):
        return pltpu.make_async_remote_copy(
            src_ref=src, dst_ref=dst.at[me], send_sem=send_sem.at[s], recv_sem=recv_sem.at[me],
            device_id=(xor(me, s),), device_id_type=MESH)

    def take(src, dst, other, send_sem, recv_sem):
        pltpu.make_async_remote_copy(
            src_ref=src, dst_ref=dst.at[other], send_sem=send_sem.at[0], recv_sem=recv_sem.at[other],
            device_id=(flip(me, 1),), device_id_type=MESH).wait_recv()

    gather_c = Gather(me, call.at[me], call, C_CHUNK, c_send, c_recv, cs_send, cs_recv)
    gather_c.stage0()
    pltpu.make_async_copy(qt_ref.at[me], in_q.at[me], q_recv.at[me]).start()
    pltpu.make_async_copy(do_ref.at[me], in_do.at[me], do_recv.at[me]).start()
    dk[...] = jnp.zeros_like(dk)
    dv[...] = jnp.zeros_like(dv)
    qz[...] = jnp.zeros_like(qz)
    dw_own[...] = jnp.zeros_like(dw_own)
    gather_c.stage1()
    gather_c.stage2()

    def send_q(s, carry):
        other = xor(me, s)
        send(qt_ref.at[other], in_q, s, q_send, q_recv).start()
        send(do_ref.at[other], in_do, s, do_send, do_recv).start()
        return carry

    lax.fori_loop(1, N, send_q, 0)
    for load in loads[:2]:
        load.wait()
    gather_c.stage3()
    gather_c.finish()

    lanes = pl.ds(pl.multiple_of(me * D, D), D)

    def make_kv(jt, carry):
        wcat = jnp.concatenate([wuk[:, lanes], wuv[:, lanes]], axis=1)
        for half in range(2):
            j = jt * 2 + half
            rows = pl.ds(half * T, T)
            kv = nn_dot(call[j, pl.ds(0, T), :], wcat)
            rt = jnp.concatenate([call[j, pl.ds(T, 32), pl.ds(0, T)], call[j, pl.ds(T, 32), pl.ds(T, T)]], axis=0)
            rtz = jnp.concatenate([rt.astype(F32), jnp.zeros((R, T), F32)], axis=0)
            kcat[jt, rows, pl.ds(0, D)] = kv[:, :D].astype(BF16)
            kcat[jt, rows, pl.ds(D, D)] = transpose(rtz).astype(BF16)
            v[jt, rows, :] = kv[:, D:].astype(BF16)
            kvt = transpose(kv).astype(BF16)
            kt[jt, pl.ds(0, D), rows] = kvt[:D]
            kt[jt, pl.ds(D, R), rows] = rt
            vt[jt, :, rows] = kvt[D:]
        return carry

    lax.fori_loop(0, NT, make_kv, 0)

    def q_step(s, carry):
        i = xor(me, s)
        take(qt_ref.at[i], in_q, i, q_send, q_recv)
        take(do_ref.at[i], in_do, i, do_send, do_recv)
        last = lax.div(i, 2)
        qz[pl.ds(0, QK), :] = in_q[i]

        def score_tile(jt, top):
            sc = nn_dot(kcat[jt], qz[...])
            sbuf[jt] = sc
            return jnp.maximum(top, fold(sc, jnp.max))

        top = lax.fori_loop(0, last, score_tile, jnp.full((8, T), -1e30, F32))
        sc = nn_dot(kcat[last], qz[...])
        ahead = lax.broadcasted_iota(jnp.int32, sc.shape, 0) - lax.broadcasted_iota(jnp.int32, sc.shape, 1)
        sc = jnp.where(ahead <= i * T - last * TK, sc, -1e30)
        sbuf[last] = sc
        top = jnp.maximum(top, fold(sc, jnp.max))
        top = jnp.max(top, axis=0, keepdims=True) * EXP_C

        ot[...] = jnp.zeros_like(ot)

        def soft_tile(jt, total):
            e = jnp.exp2(sbuf[jt] * EXP_C - top)
            sbuf[jt] = e
            ot[...] += nn_dot(vt[jt], e.astype(BF16))
            return total + fold(e, jnp.sum)

        total = lax.fori_loop(0, last + 1, soft_tile, jnp.zeros((8, T), F32))
        inv = 1.0 / jnp.sum(total, axis=0, keepdims=True)
        o_t = ot[...] * inv
        stage_o[s] = transpose(o_t).astype(BF16)

        @pl.when(s > 0)
        def _():
            send(stage_o.at[s], o_ref, s, o_send, o_recv).start()

        do_t = transpose(in_do[i].astype(F32))
        delta = jnp.sum(o_t * do_t, axis=0, keepdims=True)
        dqt[...] = jnp.zeros_like(dqt)

        def back_tile(jt, c):
            do = in_do[i]
            dp = nt_dot(v[jt], do)
            p = sbuf[jt] * inv
            ds = (p * (dp - delta)).astype(BF16)
            dv[jt] += nn_dot(p.astype(BF16), do)
            dk[jt] += nt_dot(ds, qz[...])
            dqt[...] += nn_dot(kt[jt], ds)
            return c

        lax.fori_loop(0, last + 1, back_tile, 0)
        stage_dq[s] = (dqt[...] * SCALE).astype(BF16)

        @pl.when(s > 0)
        def _():
            send(stage_dq.at[s], dq_ref, s, dq_send, dq_recv).start()

        return carry

    lax.fori_loop(0, N, q_step, 0)
    pltpu.make_async_copy(stage_o.at[0], o_ref.at[me], o_recv.at[me]).start()
    pltpu.make_async_copy(stage_dq.at[0], dq_ref.at[me], dq_recv.at[me]).start()

    def grad_kv(s, carry):
        i = xor(me, s)
        rows = pl.ds(pl.multiple_of(lax.rem(i, 2) * T, T), T)
        key = dk[lax.div(i, 2), rows, :] * SCALE
        stage_g[s, pl.ds(0, T), pl.ds(0, D)] = key[:, :D].astype(BF16)
        stage_g[s, pl.ds(0, T), pl.ds(D, D)] = dv[lax.div(i, 2), rows, :].astype(BF16)
        stage_g[s, pl.ds(T, R), :] = transpose(key[:, D:])[:R].astype(BF16)

        @pl.when(s > 0)
        def _():
            send(stage_g.at[s], in_g, s, g_send, g_recv).start()

        return carry

    lax.fori_loop(0, N, grad_kv, 0)
    pltpu.make_async_copy(stage_g.at[0], in_g.at[me], g_recv.at[me]).start()

    def grad_w(s, acc):
        both_t = transpose(stage_g[s, pl.ds(0, T), :].astype(F32)).astype(BF16)
        return acc + nn_dot(both_t, call[xor(me, s), pl.ds(0, T), :])

    dwt = lax.fori_loop(0, N, grad_w, jnp.zeros((2 * D, L), F32))
    dw_own[pl.ds(0, L), :] = transpose(dwt[:D])
    dw_own[pl.ds(L, L), :] = transpose(dwt[D:])
    own_w = pltpu.make_async_copy(dw_own, dw_ref.at[me], local_sem.at[5])
    own_w.start()
    gather_w = Gather(me, dw_own, dw_ref, W_CHUNK, w_send, w_recv, ws_send, ws_recv)
    gather_w.stage0()
    gather_w.stage1()
    gather_w.stage2()

    def take_g(h, carry):
        take(stage_g.at[0], in_g, h, g_send, g_recv)
        return carry

    lax.fori_loop(0, N, take_g, 0)

    def latent_grad(h, acc):
        cols = pl.ds(pl.multiple_of(h * D, D), D)
        wcat = jnp.concatenate([wuk[:, cols], wuv[:, cols]], axis=1)
        return acc + nt_dot(in_g[h, pl.ds(0, T), :], wcat)

    dc_ref[...] = lax.fori_loop(0, N, latent_grad, jnp.zeros((T, L), F32)).astype(BF16)

    def rope_grad(h, acc):
        return acc + in_g[h, pl.ds(T, R), :].astype(F32)

    drt_ref[...] = lax.fori_loop(0, N, rope_grad, jnp.zeros((R, T), F32)).astype(BF16)

    gather_w.stage3()
    gather_w.finish()
    own_w.wait()

    def take_o(h, carry):
        take(stage_o.at[0], o_ref, h, o_send, o_recv)
        take(stage_dq.at[0], dq_ref, h, dq_send, dq_recv)
        return carry

    lax.fori_loop(0, N, take_o, 0)

    def drain(s, carry):
        other = xor(me, s)
        send(qt_ref.at[other], in_q, s, q_send, q_recv).wait_send()
        send(do_ref.at[other], in_do, s, do_send, do_recv).wait_send()
        send(stage_o.at[s], o_ref, s, o_send, o_recv).wait_send()
        send(stage_dq.at[s], dq_ref, s, dq_send, dq_recv).wait_send()
        send(stage_g.at[s], in_g, s, g_send, g_recv).wait_send()
        return carry

    lax.fori_loop(1, N, drain, 0)
    gather_c.drain()
    gather_w.drain()


def solution(mesh):
    seq_spec = P("cp")

    def local_step(queries, latent, key_rope, w_uk, w_uv, d_out):
        any_spec = pl.BlockSpec(memory_space=pl.ANY)
        vmem_spec = pl.BlockSpec(memory_space=pltpu.VMEM)
        dma = pltpu.SemaphoreType.DMA
        o_all, dq_all, dc, drt, dw = pl.pallas_call(
            kernel,
            name="mla_core",
            out_shape=(jax.ShapeDtypeStruct((N, T, D), BF16),
                       jax.ShapeDtypeStruct((N, QK, T), BF16),
                       jax.ShapeDtypeStruct((T, L), BF16),
                       jax.ShapeDtypeStruct((R, T), BF16),
                       jax.ShapeDtypeStruct((N, 3 * W_CHUNK, D), F32)),
            in_specs=[any_spec] * 6,
            out_specs=(any_spec, any_spec, vmem_spec, vmem_spec, any_spec),
            scratch_shapes=[
                pltpu.VMEM((N, QK, T), BF16),
                pltpu.VMEM((N, T, D), BF16),
                pltpu.VMEM((N, T, D), BF16),
                pltpu.VMEM((N, QK, T), BF16),
                pltpu.VMEM((N, T + R, 2 * D), BF16),
                pltpu.VMEM((N, T + R, 2 * D), BF16),
                pltpu.VMEM((N, 3 * C_CHUNK, L), BF16),
                pltpu.VMEM((NT, TK, 2 * D), BF16),
                pltpu.VMEM((NT, QK, TK), BF16),
                pltpu.VMEM((NT, TK, D), BF16),
                pltpu.VMEM((NT, D, TK), BF16),
                pltpu.VMEM((NT, TK, T), F32),
                pltpu.VMEM((2 * D, T), BF16),
                pltpu.VMEM((NT, TK, 2 * D), F32),
                pltpu.VMEM((NT, TK, D), F32),
                pltpu.VMEM((D, T), F32),
                pltpu.VMEM((QK, T), F32),
                pltpu.VMEM((L, N * D), BF16),
                pltpu.VMEM((L, N * D), BF16),
                pltpu.VMEM((3 * W_CHUNK, D), F32),
            ] + [dma((N,))] * 10 + [dma((6,))] + [dma((24,))] * 8,
            compiler_params=pltpu.CompilerParams(
                collective_id=0, has_side_effects=True, vmem_limit_bytes=60 * 1024 * 1024),
        )(jnp.transpose(queries, (1, 2, 0)), jnp.transpose(d_out, (1, 0, 2)), latent, jnp.transpose(key_rope, (1, 0)),
          w_uk.reshape(L, N * D), w_uv.reshape(L, N * D))

        d_w = jnp.transpose(dw[:, :2 * L], (1, 0, 2))
        return (jnp.transpose(o_all, (1, 0, 2)), jnp.transpose(dq_all, (2, 0, 1)), dc, jnp.transpose(drt, (1, 0)),
                d_w[:L], d_w[L:])

    return jax.shard_map(local_step, mesh=mesh,
                         in_specs=(seq_spec, seq_spec, seq_spec, P(), P(), seq_spec),
                         out_specs=(seq_spec, seq_spec, seq_spec, seq_spec, P(), P()),
                         check_vma=False)
```

time: 824 us -> 205 us (0.25)
  the two profiles are of different devices: /device:TPU:0 before, /device:TPU:14 now
where the time goes in v1:
time: 205 us
  Pallas kernels  177 us (86%)
  local copies, waits for them, and re-layouts  27.9 us (14%)
    pallas_call x1, Pallas kernels, local_step(): pl.pallas_call(kernel, name='mla_core', out_shape=(jax.ShapeDtypeStruct((...  177 us
    unnamed x13, local copies, waits for them, and re-layouts  16.7 us
    reshape x1, local copies, waits for them, and re-layouts, local_step(): w_uv.reshape(L, N * D)  6.34 us

profile of v1, /device:TPU:14, one launch (start us, length us, event | category | flops | bytes accessed | tf_op | source)
XLA Modules:
  0.0 205.2 jit_solution(433792914754151104)
XLA Ops:
  0.6 2.5 %copy.21 = bf16[256,16,128]{2,0,1:T(8,128)(2,1)} copy(bf16[256,16,128]{2,1,0:T(8,128)(2,1)} %param.11) | data formatting | bytes 2097152 | tf_op args[5]
  3.1 6.3 %copy_bitcast_fusion = (bf16[512,2048]{1,0:T(8,128)(2,1)}, bf16[512,2048]{1,0:T(8,128)(2,1)}) fusion(bf16[64,8,16,128]{3,2,1,0:T(8,128)(2,1)} %bitcast.17, bf16[64,8,16,128]{3,2,1,0:T(8,128)(2,1)} %bitcast.18), kind=kLoop, calls=%fused_computation.1 | loop fusion | bytes 8388608 | tf_op jit(solution)/shard_map/reshape | solution.py:423
  9.4 176.6 %mla_core.1 = (bf16[16,256,128]{2,1,0:T(8,128)(2,1)}, bf16[16,192,256]{2,1,0:T(8,128)(2,1)}, bf16[256,512]{1,0:T(8,128)(2,1)}, bf16[64,256]{1,0:T(8,128)(2,1)}, f32[16,1032,128]{2,1,0:T(8,128)}) custom-call(bf16[16,192,256]{2,1,0:T(8,128)(2,1)} %bitcast.19, bf16[16,256,128]{2,1,0:T(8,128)(2,1)} %bitcast.16, bf16[256,512]{1,0:T(8,128)(2,1)} %c_ref.1, ...), custom_call_target="tpu_custom_call" | custom-call | tf_op jit(solution)/shard_map/mla_core/pallas_call | solution.py:388
  186.1 2.9 %copy.13 = bf16[256,16,128]{2,1,0:T(8,128)(2,1)} copy(bf16[256,16,128]{2,0,1:T(8,128)(2,1)} %bitcast.21) | data formatting | bytes 2097152
  188.9 4.0 %slice_bitcast_fusion = f32[1024,16,128]{2,0,1:T(8,128)S(1)} fusion(f32[16,1032,128]{2,1,0:T(8,128)} %get-tuple-element.15), kind=kLoop, calls=%fused_computation | loop fusion | bytes 16777216 | tf_op jit(solution)/shard_map/transpose | solution.py:425
  192.9 0.9 fusion
  193.8 4.4 %copy.15 = f32[512,16,128]{2,1,0:T(8,128)} copy(f32[512,16,128]{2,0,1:T(8,128)S(1)} %get-tuple-element.22) | data formatting | bytes 8388608
  198.3 0.0 copy-start
  198.3 0.0 copy-start.1
  198.3 0.0 copy-start.2
  198.3 4.4 %copy.14 = f32[512,16,128]{2,1,0:T(8,128)} copy(f32[512,16,128]{2,0,1:T(8,128)S(1)} %get-tuple-element.23) | data formatting | bytes 8388608
  202.7 0.0 copy-done
  202.7 1.1 copy.25
  203.9 0.0 copy-done.1
  203.9 0.7 copy.26
  204.6 0.0 copy-done.2
  204.6 0.6 copy.27
Async XLA Ops:
  198.3 4.5 %copy-start = (bf16[16,192,256]{2,1,0:T(8,128)(2,1)S(1)}, bf16[16,192,256]{2,1,0:T(8,128)(2,1)}, u32[]{:S(2)}) copy-start(bf16[16,192,256]{2,1,0:T(8,128)(2,1)} %get-tuple-element.12) | copy-start | bytes 4718596
  198.3 5.6 %copy-start.1 = (bf16[256,512]{1,0:T(8,128)(2,1)S(1)}, bf16[256,512]{1,0:T(8,128)(2,1)}, u32[]{:S(2)}) copy-start(bf16[256,512]{1,0:T(8,128)(2,1)} %get-tuple-element.34) | copy-start | bytes 786436
  198.3 6.3 %copy-start.2 = (bf16[64,256]{1,0:T(8,128)(2,1)S(1)}, bf16[64,256]{1,0:T(8,128)(2,1)}, u32[]{:S(2)}) copy-start(bf16[64,256]{1,0:T(8,128)(2,1)} %get-tuple-element.14) | copy-start | bytes 98308

commit v2 on v1

--- a/solution.py
+++ b/solution.py
@@ -19,7 +19,10 @@
 TK = 512
 NT = 8
 C_CHUNK = 96
-W_CHUNK = 344
+W_CHUNK = 176
+NP = 72
+ORDER = (0, 7, 3, 4, 5, 2, 6, 1)
+TABLE = sum(chip << (3 * n) for n, chip in enumerate(ORDER))
 SCALE = 1.0 / math.sqrt(QK)
 EXP_C = SCALE * math.log2(math.e)
 
@@ -43,6 +46,12 @@
     return x
 
 
+def partner(n):
+    k = lax.div(n, 2)
+    power = (1 + 7 * lax.rem(k, 2)) * (1 + 63 * lax.rem(lax.div(k, 2), 2)) * (1 + 4095 * lax.div(k, 4))
+    return 2 * lax.rem(lax.div(TABLE, power), 8) + lax.rem(n, 2)
+
+
 def fold(x, reduce):
     return reduce(x.reshape(x.shape[0] // 8, 8, x.shape[1]), axis=0)
 
@@ -52,8 +61,8 @@
 
 
 class Gather:
-    def __init__(self, me, own, buf, chunk, send_sem, recv_sem, sib_send, sib_recv):
-        self.me, self.own, self.buf, self.chunk = me, own, buf, chunk
+    def __init__(self, me, own, view, chunk, send_sem, recv_sem, sib_send, sib_recv):
+        self.me, self.own, self.view, self.chunk = me, own, view, chunk
         self.send_sem, self.recv_sem = send_sem, recv_sem
         self.sib_send, self.sib_recv = sib_send, sib_recv
 
@@ -70,9 +79,9 @@
             src = flip(src, bit)
         rows = pl.ds(k * self.chunk, self.chunk)
         slot = k * 8 + lax.div(mask, 2)
-        first = self.own.at[rows, :] if not masks else self.buf.at[src, rows, :]
+        first = self.own.at[rows, :] if not masks else self.view(src, rows)
         return pltpu.make_async_remote_copy(
-            src_ref=first, dst_ref=self.buf.at[src, rows, :], send_sem=send_sem.at[slot], recv_sem=recv_sem.at[slot],
+            src_ref=first, dst_ref=self.view(src, rows), send_sem=send_sem.at[slot], recv_sem=recv_sem.at[slot],
             device_id=(target,), device_id_type=MESH)
 
     def hop(self, k, masks, bit):
@@ -133,7 +142,7 @@
         def step(n, carry):
             k, half = lax.div(n, 8), lax.rem(n, 8)
             rows = pl.ds(k * self.chunk, self.chunk)
-            ref = self.buf.at[xor(sibling, 2 * half), rows, :]
+            ref = self.view(xor(sibling, 2 * half), rows)
             pltpu.make_async_remote_copy(
                 src_ref=ref, dst_ref=ref, send_sem=self.sib_send.at[n], recv_sem=self.sib_recv.at[n],
                 device_id=(sibling,), device_id_type=MESH).wait_recv()
@@ -144,7 +153,7 @@
         def step(n, carry):
             k, half = lax.div(n, 8), lax.rem(n, 8)
             rows = pl.ds(k * self.chunk, self.chunk)
-            ref = self.buf.at[xor(self.me, 2 * half), rows, :]
+            ref = self.view(xor(self.me, 2 * half), rows)
             pltpu.make_async_remote_copy(
                 src_ref=ref, dst_ref=ref, send_sem=self.sib_send.at[n], recv_sem=self.sib_recv.at[n],
                 device_id=(flip(self.me, 1),), device_id_type=MESH).wait_send()
@@ -159,10 +168,11 @@
 
 
 def kernel(qt_ref, do_ref, c_ref, rt_ref, wuk_ref, wuv_ref,
-           o_ref, dq_ref, dc_ref, drt_ref, dw_ref,
-           in_q, in_do, stage_o, stage_dq, stage_g, in_g, call, kcat, kt, v, vt, sbuf, qz, dk, dv, ot, dqt, wuk, wuv, dw_own,
-           q_send, q_recv, do_send, do_recv, o_send, o_recv, dq_send, dq_recv, g_send, g_recv, local_sem,
-           c_send, c_recv, cs_send, cs_recv, w_send, w_recv, ws_send, ws_recv):
+           o_ref, dq_ref, dc_ref, drt_ref, dwk_ref, dwv_ref,
+           in_q, in_do, stage_o, stage_dq, stage_v, stage_k, in_v, in_k, call, kcat, kt, v, vt, sbuf, prob, qz, dk, dv,
+           ot, dqt, delta, dct, wuk, wuv, dwk_own, dwv_own,
+           q_send, q_recv, do_send, do_recv, o_send, o_recv, dq_send, dq_recv, v_send, v_recv, k_send, k_recv, local_sem,
+           c_send, c_recv, cs_send, cs_recv, gk_send, gk_recv, gks_send, gks_recv, gv_send, gv_recv, gvs_send, gvs_recv):
     me = lax.axis_index("cp")
 
     loads = [
@@ -186,31 +196,32 @@
         load.wait()
     pl.semaphore_wait(barrier, N - 1)
 
-    def send(src, dst, s, send_sem, recv_sem):
+    def send(src, dst, n, send_sem, recv_sem):
         return pltpu.make_async_remote_copy(
-            src_ref=src, dst_ref=dst.at[me], send_sem=send_sem.at[s], recv_sem=recv_sem.at[me],
-            device_id=(xor(me, s),), device_id_type=MESH)
+            src_ref=src, dst_ref=dst.at[me], send_sem=send_sem.at[n], recv_sem=recv_sem.at[me],
+            device_id=(xor(me, partner(n)),), device_id_type=MESH)
 
     def take(src, dst, other, send_sem, recv_sem):
         pltpu.make_async_remote_copy(
             src_ref=src, dst_ref=dst.at[other], send_sem=send_sem.at[0], recv_sem=recv_sem.at[other],
             device_id=(flip(me, 1),), device_id_type=MESH).wait_recv()
 
-    gather_c = Gather(me, call.at[me], call, C_CHUNK, c_send, c_recv, cs_send, cs_recv)
+    gather_c = Gather(me, call.at[me], lambda src, rows: call.at[src, rows, :], C_CHUNK, c_send, c_recv, cs_send, cs_recv)
     gather_c.stage0()
     pltpu.make_async_copy(qt_ref.at[me], in_q.at[me], q_recv.at[me]).start()
     pltpu.make_async_copy(do_ref.at[me], in_do.at[me], do_recv.at[me]).start()
     dk[...] = jnp.zeros_like(dk)
     dv[...] = jnp.zeros_like(dv)
     qz[...] = jnp.zeros_like(qz)
-    dw_own[...] = jnp.zeros_like(dw_own)
+    dwk_own[...] = jnp.zeros_like(dwk_own)
+    dwv_own[...] = jnp.zeros_like(dwv_own)
     gather_c.stage1()
     gather_c.stage2()
 
-    def send_q(s, carry):
-        other = xor(me, s)
-        send(qt_ref.at[other], in_q, s, q_send, q_recv).start()
-        send(do_ref.at[other], in_do, s, do_send, do_recv).start()
+    def send_q(n, carry):
+        other = xor(me, partner(n))
+        send(qt_ref.at[other], in_q, n, q_send, q_recv).start()
+        send(do_ref.at[other], in_do, n, do_send, do_recv).start()
         return carry
 
     lax.fori_loop(1, N, send_q, 0)
@@ -240,11 +251,16 @@
 
     lax.fori_loop(0, NT, make_kv, 0)
 
-    def q_step(s, carry):
-        i = xor(me, s)
+    def first_prob(i):
+        half = lax.div(i, 2)
+        return (half + lax.rem(i, 2)) * (half + 1)
+
+    def forward(n, carry):
+        i = xor(me, partner(n))
         take(qt_ref.at[i], in_q, i, q_send, q_recv)
         take(do_ref.at[i], in_do, i, do_send, do_recv)
         last = lax.div(i, 2)
+        base = first_prob(i)
         qz[pl.ds(0, QK), :] = in_q[i]
 
         def score_tile(jt, top):
@@ -271,91 +287,146 @@
         total = lax.fori_loop(0, last + 1, soft_tile, jnp.zeros((8, T), F32))
         inv = 1.0 / jnp.sum(total, axis=0, keepdims=True)
         o_t = ot[...] * inv
-        stage_o[s] = transpose(o_t).astype(BF16)
-
-        @pl.when(s > 0)
+        stage_o[n] = transpose(o_t).astype(BF16)
+
+        @pl.when(n > 0)
         def _():
-            send(stage_o.at[s], o_ref, s, o_send, o_recv).start()
+            send(stage_o.at[n], o_ref, n, o_send, o_recv).start()
 
         do_t = transpose(in_do[i].astype(F32))
-        delta = jnp.sum(o_t * do_t, axis=0, keepdims=True)
+        delta[n] = jnp.broadcast_to(jnp.sum(o_t * do_t, axis=0, keepdims=True), (8, T))
+
+        def value_tile(jt, c):
+            p = (sbuf[jt] * inv).astype(BF16)
+            prob[base + jt] = p
+            dv[jt] += nn_dot(p, in_do[i])
+            return c
+
+        lax.fori_loop(0, last + 1, value_tile, 0)
+        return carry
+
+    lax.fori_loop(0, N, forward, 0)
+    pltpu.make_async_copy(stage_o.at[0], o_ref.at[me], o_recv.at[me]).start()
+
+    def block_rows(i):
+        return pl.ds(pl.multiple_of(lax.rem(i, 2) * T, T), T)
+
+    def grad_v(n, carry):
+        i = xor(me, partner(n))
+        stage_v[n] = transpose(dv[lax.div(i, 2), block_rows(i), :]).astype(BF16)
+
+        @pl.when(n > 0)
+        def _():
+            send(stage_v.at[n], in_v, n, v_send, v_recv).start()
+
+        return carry
+
+    def weight_grad(stage, own):
+        def step(m, acc):
+            lhs = jnp.concatenate([stage[4 * m + r, pl.ds(0, D), :] for r in range(4)], axis=1)
+            rhs = jnp.concatenate([call[xor(me, partner(4 * m + r)), pl.ds(0, T), :] for r in range(4)], axis=0)
+            return acc + nn_dot(lhs, rhs)
+
+        dwt = lax.fori_loop(0, 4, step, jnp.zeros((D, L), F32))
+        own[pl.ds(0, L), :] = transpose(dwt)
+
+    lax.fori_loop(0, N, grad_v, 0)
+    pltpu.make_async_copy(stage_v.at[0], in_v.at[me], v_recv.at[me]).start()
+    weight_grad(stage_v, dwv_own)
+    gather_v = Gather(me, dwv_own, lambda src, rows: dwv_ref.at[rows, src, 0, :], W_CHUNK, gv_send, gv_recv, gvs_send, gvs_recv)
+    all_rows = pl.ds(0, 3 * W_CHUNK)
+    own_v = pltpu.make_async_copy(dwv_own, gather_v.view(me, all_rows), local_sem.at[5])
+    own_v.start()
+    gather_v.stage0()
+
+    def backward(n, carry):
+        i = xor(me, partner(n))
+        last = lax.div(i, 2)
+        base = first_prob(i)
+        qz[pl.ds(0, QK), :] = in_q[i]
         dqt[...] = jnp.zeros_like(dqt)
+        row_delta = delta[n, pl.ds(0, 1), :]
 
         def back_tile(jt, c):
-            do = in_do[i]
-            dp = nt_dot(v[jt], do)
-            p = sbuf[jt] * inv
-            ds = (p * (dp - delta)).astype(BF16)
-            dv[jt] += nn_dot(p.astype(BF16), do)
+            dp = nt_dot(v[jt], in_do[i])
+            ds = (prob[base + jt].astype(F32) * (dp - row_delta)).astype(BF16)
             dk[jt] += nt_dot(ds, qz[...])
             dqt[...] += nn_dot(kt[jt], ds)
             return c
 
         lax.fori_loop(0, last + 1, back_tile, 0)
-        stage_dq[s] = (dqt[...] * SCALE).astype(BF16)
-
-        @pl.when(s > 0)
+        stage_dq[n] = (dqt[...] * SCALE).astype(BF16)
+
+        @pl.when(n > 0)
         def _():
-            send(stage_dq.at[s], dq_ref, s, dq_send, dq_recv).start()
-
-        return carry
-
-    lax.fori_loop(0, N, q_step, 0)
-    pltpu.make_async_copy(stage_o.at[0], o_ref.at[me], o_recv.at[me]).start()
+            send(stage_dq.at[n], dq_ref, n, dq_send, dq_recv).start()
+
+        @pl.when(n == 4)
+        def _():
+            gather_v.stage1()
+
+        @pl.when(n == 8)
+        def _():
+            gather_v.stage2()
+
+        @pl.when(n == 12)
+        def _():
+            gather_v.stage3()
+
+        return carry
+
+    lax.fori_loop(0, N, backward, 0)
     pltpu.make_async_copy(stage_dq.at[0], dq_ref.at[me], dq_recv.at[me]).start()
 
-    def grad_kv(s, carry):
-        i = xor(me, s)
-        rows = pl.ds(pl.multiple_of(lax.rem(i, 2) * T, T), T)
-        key = dk[lax.div(i, 2), rows, :] * SCALE
-        stage_g[s, pl.ds(0, T), pl.ds(0, D)] = key[:, :D].astype(BF16)
-        stage_g[s, pl.ds(0, T), pl.ds(D, D)] = dv[lax.div(i, 2), rows, :].astype(BF16)
-        stage_g[s, pl.ds(T, R), :] = transpose(key[:, D:])[:R].astype(BF16)
-
-        @pl.when(s > 0)
-        def _():
-            send(stage_g.at[s], in_g, s, g_send, g_recv).start()
-
-        return carry
-
-    lax.fori_loop(0, N, grad_kv, 0)
-    pltpu.make_async_copy(stage_g.at[0], in_g.at[me], g_recv.at[me]).start()
-
-    def grad_w(s, acc):
-        both_t = transpose(stage_g[s, pl.ds(0, T), :].astype(F32)).astype(BF16)
-        return acc + nn_dot(both_t, call[xor(me, s), pl.ds(0, T), :])
-
-    dwt = lax.fori_loop(0, N, grad_w, jnp.zeros((2 * D, L), F32))
-    dw_own[pl.ds(0, L), :] = transpose(dwt[:D])
-    dw_own[pl.ds(L, L), :] = transpose(dwt[D:])
-    own_w = pltpu.make_async_copy(dw_own, dw_ref.at[me], local_sem.at[5])
-    own_w.start()
-    gather_w = Gather(me, dw_own, dw_ref, W_CHUNK, w_send, w_recv, ws_send, ws_recv)
-    gather_w.stage0()
-    gather_w.stage1()
-    gather_w.stage2()
-
-    def take_g(h, carry):
-        take(stage_g.at[0], in_g, h, g_send, g_recv)
-        return carry
-
-    lax.fori_loop(0, N, take_g, 0)
-
-    def latent_grad(h, acc):
+    def grad_k(n, carry):
+        i = xor(me, partner(n))
+        key = transpose(dk[lax.div(i, 2), block_rows(i), :] * SCALE)
+        stage_k[n] = key[:QK].astype(BF16)
+        return carry
+
+    lax.fori_loop(0, N, grad_k, 0)
+    pltpu.make_async_copy(stage_k.at[0], in_k.at[me], k_recv.at[me]).start()
+
+    def send_k(n, carry):
+        send(stage_k.at[n], in_k, n, k_send, k_recv).start()
+        return carry
+
+    lax.fori_loop(1, 4, send_k, 0)
+    weight_grad(stage_k, dwk_own)
+    gather_k = Gather(me, dwk_own, lambda src, rows: dwk_ref.at[rows, src, 0, :], W_CHUNK, gk_send, gk_recv, gks_send, gks_recv)
+    own_k = pltpu.make_async_copy(dwk_own, gather_k.view(me, all_rows), local_sem.at[6])
+    own_k.start()
+    gather_k.stage0()
+    lax.fori_loop(4, 8, send_k, 0)
+
+    dct[...] = jnp.zeros_like(dct)
+
+    def latent_from_v(h, carry):
+        take(stage_v.at[0], in_v, h, v_send, v_recv)
         cols = pl.ds(pl.multiple_of(h * D, D), D)
-        wcat = jnp.concatenate([wuk[:, cols], wuv[:, cols]], axis=1)
-        return acc + nt_dot(in_g[h, pl.ds(0, T), :], wcat)
-
-    dc_ref[...] = lax.fori_loop(0, N, latent_grad, jnp.zeros((T, L), F32)).astype(BF16)
-
-    def rope_grad(h, acc):
-        return acc + in_g[h, pl.ds(T, R), :].astype(F32)
-
-    drt_ref[...] = lax.fori_loop(0, N, rope_grad, jnp.zeros((R, T), F32)).astype(BF16)
-
-    gather_w.stage3()
-    gather_w.finish()
-    own_w.wait()
+        dct[...] += nn_dot(wuv[:, cols], in_v[h])
+        return carry
+
+    lax.fori_loop(0, N, latent_from_v, 0)
+    gather_k.stage1()
+    lax.fori_loop(8, N, send_k, 0)
+    gather_k.stage2()
+
+    def latent_from_k(n, acc):
+        h = xor(me, partner(n))
+        take(stage_k.at[0], in_k, h, k_send, k_recv)
+        cols = pl.ds(pl.multiple_of(h * D, D), D)
+        dct[...] += nn_dot(wuk[:, cols], in_k[h, pl.ds(0, D), :])
+        return acc + in_k[h, pl.ds(D, R), :].astype(F32)
+
+    drt_ref[...] = lax.fori_loop(0, N, latent_from_k, jnp.zeros((R, T), F32)).astype(BF16)
+    dc_ref[...] = transpose(dct[...]).astype(BF16)
+
+    gather_k.stage3()
+    gather_v.finish()
+    gather_k.finish()
+    own_v.wait()
+    own_k.wait()
 
     def take_o(h, carry):
         take(stage_o.at[0], o_ref, h, o_send, o_recv)
@@ -364,18 +435,20 @@
 
     lax.fori_loop(0, N, take_o, 0)
 
-    def drain(s, carry):
-        other = xor(me, s)
-        send(qt_ref.at[other], in_q, s, q_send, q_recv).wait_send()
-        send(do_ref.at[other], in_do, s, do_send, do_recv).wait_send()
-        send(stage_o.at[s], o_ref, s, o_send, o_recv).wait_send()
-        send(stage_dq.at[s], dq_ref, s, dq_send, dq_recv).wait_send()
-        send(stage_g.at[s], in_g, s, g_send, g_recv).wait_send()
+    def drain(n, carry):
+        other = xor(me, partner(n))
+        send(qt_ref.at[other], in_q, n, q_send, q_recv).wait_send()
+        send(do_ref.at[other], in_do, n, do_send, do_recv).wait_send()
+        send(stage_o.at[n], o_ref, n, o_send, o_recv).wait_send()
+        send(stage_dq.at[n], dq_ref, n, dq_send, dq_recv).wait_send()
+        send(stage_v.at[n], in_v, n, v_send, v_recv).wait_send()
+        send(stage_k.at[n], in_k, n, k_send, k_recv).wait_send()
         return carry
 
     lax.fori_loop(1, N, drain, 0)
     gather_c.drain()
-    gather_w.drain()
+    gather_v.drain()
+    gather_k.drain()
 
 
 def solution(mesh):
@@ -385,46 +458,52 @@
         any_spec = pl.BlockSpec(memory_space=pl.ANY)
         vmem_spec = pl.BlockSpec(memory_space=pltpu.VMEM)
         dma = pltpu.SemaphoreType.DMA
-        o_all, dq_all, dc, drt, dw = pl.pallas_call(
+        o_all, dq_all, dc, drt, dwk, dwv = pl.pallas_call(
             kernel,
             name="mla_core",
             out_shape=(jax.ShapeDtypeStruct((N, T, D), BF16),
                        jax.ShapeDtypeStruct((N, QK, T), BF16),
                        jax.ShapeDtypeStruct((T, L), BF16),
                        jax.ShapeDtypeStruct((R, T), BF16),
-                       jax.ShapeDtypeStruct((N, 3 * W_CHUNK, D), F32)),
+                       jax.ShapeDtypeStruct((3 * W_CHUNK, N, 1, D), F32),
+                       jax.ShapeDtypeStruct((3 * W_CHUNK, N, 1, D), F32)),
             in_specs=[any_spec] * 6,
-            out_specs=(any_spec, any_spec, vmem_spec, vmem_spec, any_spec),
+            out_specs=(any_spec, any_spec, vmem_spec, vmem_spec, any_spec, any_spec),
             scratch_shapes=[
                 pltpu.VMEM((N, QK, T), BF16),
                 pltpu.VMEM((N, T, D), BF16),
                 pltpu.VMEM((N, T, D), BF16),
                 pltpu.VMEM((N, QK, T), BF16),
-                pltpu.VMEM((N, T + R, 2 * D), BF16),
-                pltpu.VMEM((N, T + R, 2 * D), BF16),
+                pltpu.VMEM((N, D, T), BF16),
+                pltpu.VMEM((N, QK, T), BF16),
+                pltpu.VMEM((N, D, T), BF16),
+                pltpu.VMEM((N, QK, T), BF16),
                 pltpu.VMEM((N, 3 * C_CHUNK, L), BF16),
                 pltpu.VMEM((NT, TK, 2 * D), BF16),
                 pltpu.VMEM((NT, QK, TK), BF16),
                 pltpu.VMEM((NT, TK, D), BF16),
                 pltpu.VMEM((NT, D, TK), BF16),
                 pltpu.VMEM((NT, TK, T), F32),
+                pltpu.VMEM((NP, TK, T), BF16),
                 pltpu.VMEM((2 * D, T), BF16),
                 pltpu.VMEM((NT, TK, 2 * D), F32),
                 pltpu.VMEM((NT, TK, D), F32),
                 pltpu.VMEM((D, T), F32),
                 pltpu.VMEM((QK, T), F32),
+                pltpu.VMEM((N, 8, T), F32),
+                pltpu.VMEM((L, T), F32),
                 pltpu.VMEM((L, N * D), BF16),
                 pltpu.VMEM((L, N * D), BF16),
                 pltpu.VMEM((3 * W_CHUNK, D), F32),
-            ] + [dma((N,))] * 10 + [dma((6,))] + [dma((24,))] * 8,
+                pltpu.VMEM((3 * W_CHUNK, D), F32),
+            ] + [dma((N,))] * 12 + [dma((7,))] + [dma((24,))] * 12,
             compiler_params=pltpu.CompilerParams(
-                collective_id=0, has_side_effects=True, vmem_limit_bytes=60 * 1024 * 1024),
+                collective_id=0, has_side_effects=True, vmem_limit_bytes=67043328),
         )(jnp.transpose(queries, (1, 2, 0)), jnp.transpose(d_out, (1, 0, 2)), latent, jnp.transpose(key_rope, (1, 0)),
           w_uk.reshape(L, N * D), w_uv.reshape(L, N * D))
 
-        d_w = jnp.transpose(dw[:, :2 * L], (1, 0, 2))
         return (jnp.transpose(o_all, (1, 0, 2)), jnp.transpose(dq_all, (2, 0, 1)), dc, jnp.transpose(drt, (1, 0)),
-                d_w[:L], d_w[L:])
+                dwk[:L].reshape(L, N, D), dwv[:L].reshape(L, N, D))
 
     return jax.shard_map(local_step, mesh=mesh,
                          in_specs=(seq_spec, seq_spec, seq_spec, P(), P(), seq_spec),

time: 205 us -> 211 us (1.029)
  the two profiles are of different devices: /device:TPU:14 before, /device:TPU:0 now
where the time goes in v2:
time: 211 us
  Pallas kernels  185 us (88%)
  local copies, waits for them, and re-layouts  25.8 us (12%)
    pallas_call x1, Pallas kernels, local_step(): pl.pallas_call(kernel, name='mla_core', out_shape=(jax.ShapeDtypeStruct((...  185 us
    unnamed x17, local copies, waits for them, and re-layouts  8.12 us
    slice x1, local copies, waits for them, and re-layouts, local_step(): dwk[:L].reshape(L, N, D)  7.11 us
    reshape x1, local copies, waits for them, and re-layouts, local_step(): w_uv.reshape(L, N * D)  5.71 us
    slice x1, local copies, waits for them, and re-layouts, local_step(): dwv[:L].reshape(L, N, D)  4.89 us

profile of v2, /device:TPU:0, one launch (start us, length us, event | category | flops | bytes accessed | tf_op | source)
XLA Modules:
  0.0 211.3 jit_solution(14068753887980152897)
XLA Ops:
  0.6 0.0 copy-start
  0.6 2.6 %copy.19 = bf16[256,16,128]{2,0,1:T(8,128)(2,1)} copy(bf16[256,16,128]{2,1,0:T(8,128)(2,1)} %param.11) | data formatting | bytes 2097152 | tf_op args[5]
  3.3 0.0 copy-done
  3.3 5.7 %copy_bitcast_fusion = (bf16[512,2048]{1,0:T(8,128)(2,1)}, bf16[512,2048]{1,0:T(8,128)(2,1)}) fusion(bf16[64,8,16,128]{3,2,1,0:T(8,128)(2,1)S(1)} %bitcast.21, bf16[64,8,16,128]{3,2,1,0:T(8,128)(2,1)} %bitcast.22), kind=kLoop, calls=%fused_computation | loop fusion | bytes 8388608 | tf_op jit(solution)/shard_map/reshape | solution.py:503
  9.0 184.8 %mla_core.1 = (bf16[16,256,128]{2,1,0:T(8,128)(2,1)}, bf16[16,192,256]{2,1,0:T(8,128)(2,1)}, bf16[256,512]{1,0:T(8,128)(2,1)}, bf16[64,256]{1,0:T(8,128)(2,1)}, ...) custom-call(bf16[16,192,256]{2,1,0:T(8,128)(2,1)} %bitcast.23, bf16[16,256,128]{2,1,0:T(8,128)(2,1)} %bitcast.16, ...), custom_call_target="tpu_custom_call" | custom-call | tf_op jit(solution)/shard_map/mla_core/pallas_call | solution.py:461
  193.8 0.0 slice-start
  193.8 3.0 %copy.13 = bf16[256,16,128]{2,1,0:T(8,128)(2,1)} copy(bf16[256,16,128]{2,0,1:T(8,128)(2,1)} %bitcast.25) | data formatting | bytes 2097152
  196.8 0.0 slice-start.1
  196.8 7.1 %slice.6 = f32[512,16,1,128]{3,2,1,0:T(1,128)} slice(f32[528,16,1,128]{3,2,1,0:T(1,128)} %get-tuple-element.16), slice={[0:512], [0:16], [0:1], [0:128]} | slice | bytes 8388608 | tf_op jit(solution)/shard_map/slice | solution.py:506
  203.9 0.0 slice-done
  203.9 0.0 slice-done.1
  203.9 0.0 copy-start.1
  203.9 4.9 %slice.7 = f32[512,16,1,128]{3,2,1,0:T(1,128)} slice(f32[528,16,1,128]{3,2,1,0:T(1,128)S(1)} %bitcast.20), slice={[0:512], [0:16], [0:1], [0:128]} | slice | bytes 8388608 | tf_op jit(solution)/shard_map/slice | solution.py:506
  208.8 0.0 copy-start.2
  208.8 0.0 copy-start.3
  208.8 0.0 copy-done.1
  208.8 1.1 copy.23
  210.0 0.0 copy-done.2
  210.0 0.7 copy.24
  210.7 0.0 copy-done.3
  210.7 0.6 copy.25
  (1 shorter events, 0.0 us)
Async XLA Ops:
  0.6 2.6 %copy-start = (bf16[512,16,128]{2,1,0:T(8,128)(2,1)S(1)}, bf16[512,16,128]{2,1,0:T(8,128)(2,1)}, u32[]{:S(2)}) copy-start(bf16[512,16,128]{2,1,0:T(8,128)(2,1)} %param.10) | copy-start | bytes 6291460
  193.8 10.1 %slice-start = ((s8[4325376]{0:T(1024)(128)(4,1)}), s8[4194304]{0:T(1024)(128)(4,1)S(1)}, s32[]{:S(2)}) async-start(s8[4325376]{0:T(1024)(128)(4,1)} %bitcast.19), calls=%async_computation | async-start | bytes 8388608
  196.8 7.1 %slice-start.1 = ((s8[4325376]{0:T(1024)(128)(4,1)}), s8[131072]{0:T(1024)(128)(4,1)S(1)}, s32[]{:S(2)}) async-start(s8[4325376]{0:T(1024)(128)(4,1)} %bitcast.19), calls=%async_computation.1 | async-start | bytes 262144
  203.9 4.9 %copy-start.1 = (bf16[16,192,256]{2,1,0:T(8,128)(2,1)S(1)}, bf16[16,192,256]{2,1,0:T(8,128)(2,1)}, u32[]{:S(2)}) copy-start(bf16[16,192,256]{2,1,0:T(8,128)(2,1)} %get-tuple-element.13) | copy-start | bytes 4718596
  208.8 1.2 copy-start.2
  208.8 1.9 copy-start.3

commit v3 on v2

--- a/solution.py
+++ b/solution.py
@@ -333,7 +333,7 @@
     lax.fori_loop(0, N, grad_v, 0)
     pltpu.make_async_copy(stage_v.at[0], in_v.at[me], v_recv.at[me]).start()
     weight_grad(stage_v, dwv_own)
-    gather_v = Gather(me, dwv_own, lambda src, rows: dwv_ref.at[rows, src, 0, :], W_CHUNK, gv_send, gv_recv, gvs_send, gvs_recv)
+    gather_v = Gather(me, dwv_own, lambda src, rows: dwv_ref.at[src, rows, :], W_CHUNK, gv_send, gv_recv, gvs_send, gvs_recv)
     all_rows = pl.ds(0, 3 * W_CHUNK)
     own_v = pltpu.make_async_copy(dwv_own, gather_v.view(me, all_rows), local_sem.at[5])
     own_v.start()
@@ -393,7 +393,7 @@
 
     lax.fori_loop(1, 4, send_k, 0)
     weight_grad(stage_k, dwk_own)
-    gather_k = Gather(me, dwk_own, lambda src, rows: dwk_ref.at[rows, src, 0, :], W_CHUNK, gk_send, gk_recv, gks_send, gks_recv)
+    gather_k = Gather(me, dwk_own, lambda src, rows: dwk_ref.at[src, rows, :], W_CHUNK, gk_send, gk_recv, gks_send, gks_recv)
     own_k = pltpu.make_async_copy(dwk_own, gather_k.view(me, all_rows), local_sem.at[6])
     own_k.start()
     gather_k.stage0()
@@ -465,8 +465,8 @@
                        jax.ShapeDtypeStruct((N, QK, T), BF16),
                        jax.ShapeDtypeStruct((T, L), BF16),
                        jax.ShapeDtypeStruct((R, T), BF16),
-                       jax.ShapeDtypeStruct((3 * W_CHUNK, N, 1, D), F32),
-                       jax.ShapeDtypeStruct((3 * W_CHUNK, N, 1, D), F32)),
+                       jax.ShapeDtypeStruct((N, 3 * W_CHUNK, D), F32),
+                       jax.ShapeDtypeStruct((N, 3 * W_CHUNK, D), F32)),
             in_specs=[any_spec] * 6,
             out_specs=(any_spec, any_spec, vmem_spec, vmem_spec, any_spec, any_spec),
             scratch_shapes=[
@@ -503,7 +503,7 @@
           w_uk.reshape(L, N * D), w_uv.reshape(L, N * D))
 
         return (jnp.transpose(o_all, (1, 0, 2)), jnp.transpose(dq_all, (2, 0, 1)), dc, jnp.transpose(drt, (1, 0)),
-                dwk[:L].reshape(L, N, D), dwv[:L].reshape(L, N, D))
+                jnp.transpose(dwk[:, :L], (1, 0, 2)), jnp.transpose(dwv[:, :L], (1, 0, 2)))
 
     return jax.shard_map(local_step, mesh=mesh,
                          in_specs=(seq_spec, seq_spec, seq_spec, P(), P(), seq_spec),

time: 211 us -> 211 us (level)
    unnamed x17, local copies, waits for them, and re-layouts: 8.12 us -> 22.2 us
    slice x2 -> x0, local copies, waits for them, and re-layouts: 12 us -> none  [the longest x1 7.11 us: local_step(): dwk[:L].reshape(L, N, D)]
    reshape x1 -> x0, local copies, waits for them, and re-layouts: 5.71 us -> none  [local_step(): w_uv.reshape(L, N * D)]
    transpose x0 -> x1, local copies, waits for them, and re-layouts: none -> 4.04 us  [local_step(): jnp.transpose(dwv[:, :L], (1, 0, 2))]
where the time goes in v3:
time: 211 us
  Pallas kernels  184 us (87%)
  local copies, waits for them, and re-layouts  26.2 us (12%)
    pallas_call x1, Pallas kernels, local_step(): pl.pallas_call(kernel, name='mla_core', out_shape=(jax.ShapeDtypeStruct((...  184 us
    unnamed x17, local copies, waits for them, and re-layouts  22.2 us

profile of v3, /device:TPU:0, one launch (start us, length us, event | category | flops | bytes accessed | tf_op | source)
XLA Modules:
  0.0 211.0 jit_solution(13420631771408617614)
XLA Ops:
  0.6 0.0 copy-start
  0.6 2.6 %copy.23 = bf16[256,16,128]{2,0,1:T(8,128)(2,1)} copy(bf16[256,16,128]{2,1,0:T(8,128)(2,1)} %param.11) | data formatting | bytes 2097152 | tf_op args[5]
  3.3 3.5 %copy.22 = bf16[64,8,16,128]{3,1,2,0:T(8,128)(2,1)} copy(bf16[64,8,16,128]{3,2,1,0:T(8,128)(2,1)} %bitcast.23) | data formatting | bytes 4194304
  6.7 0.0 copy-done
  6.7 1.9 copy.21
  8.6 184.1 %mla_core.1 = (bf16[16,256,128]{2,1,0:T(8,128)(2,1)}, bf16[16,192,256]{2,1,0:T(8,128)(2,1)}, bf16[256,512]{1,0:T(8,128)(2,1)}, bf16[64,256]{1,0:T(8,128)(2,1)}, ...) custom-call(bf16[16,192,256]{2,1,0:T(8,128)(2,1)} %bitcast.25, bf16[16,256,128]{2,1,0:T(8,128)(2,1)} %bitcast.22, ...), custom_call_target="tpu_custom_call" | custom-call | tf_op jit(solution)/shard_map/mla_core/pallas_call | solution.py:461
  192.7 2.9 %copy.13 = bf16[256,16,128]{2,1,0:T(8,128)(2,1)} copy(bf16[256,16,128]{2,0,1:T(8,128)(2,1)} %bitcast.27) | data formatting | bytes 2097152
  195.6 4.0 %slice_bitcast_fusion = (f32[512,16,128]{2,0,1:T(8,128)S(1)}, f32[512,16,128]{2,0,1:T(8,128)S(1)}) fusion(f32[16,528,128]{2,1,0:T(8,128)} %get-tuple-element.17, f32[16,528,128]{2,1,0:T(8,128)} %get-tuple-element.16), kind=kLoop, calls=%fused_computation | loop fusion | bytes 16777216 | tf_op jit(solution)/shard_map/transpose | solution.py:506
  199.6 4.4 %copy.15 = f32[512,16,128]{2,1,0:T(8,128)} copy(f32[512,16,128]{2,0,1:T(8,128)S(1)} %get-tuple-element.24) | data formatting | bytes 8388608
  204.1 0.0 copy-start.1
  204.1 0.0 copy-start.2
  204.1 0.0 copy-start.3
  204.1 4.4 %copy.14 = f32[512,16,128]{2,1,0:T(8,128)} copy(f32[512,16,128]{2,0,1:T(8,128)S(1)} %get-tuple-element.25) | data formatting | bytes 8388608
  208.5 0.0 copy-done.1
  208.5 1.1 copy.27
  209.7 0.0 copy-done.2
  209.7 0.7 copy.28
  210.4 0.0 copy-done.3
  210.4 0.6 copy.29
Async XLA Ops:
  0.6 6.1 %copy-start = (bf16[512,16,128]{2,1,0:T(8,128)(2,1)S(1)}, bf16[512,16,128]{2,1,0:T(8,128)(2,1)}, u32[]{:S(2)}) copy-start(bf16[512,16,128]{2,1,0:T(8,128)(2,1)} %param.10) | copy-start | bytes 6291460
  204.1 4.5 %copy-start.1 = (bf16[16,192,256]{2,1,0:T(8,128)(2,1)S(1)}, bf16[16,192,256]{2,1,0:T(8,128)(2,1)}, u32[]{:S(2)}) copy-start(bf16[16,192,256]{2,1,0:T(8,128)(2,1)} %get-tuple-element.13) | copy-start | bytes 4718596
  204.1 5.6 %copy-start.2 = (bf16[256,512]{1,0:T(8,128)(2,1)S(1)}, bf16[256,512]{1,0:T(8,128)(2,1)}, u32[]{:S(2)}) copy-start(bf16[256,512]{1,0:T(8,128)(2,1)} %get-tuple-element.34) | copy-start | bytes 786436
  204.1 6.3 %copy-start.3 = (bf16[64,256]{1,0:T(8,128)(2,1)S(1)}, bf16[64,256]{1,0:T(8,128)(2,1)}, u32[]{:S(2)}) copy-start(bf16[64,256]{1,0:T(8,128)(2,1)} %get-tuple-element.15) | copy-start | bytes 98308

commit v4 on v3

--- a/solution.py
+++ b/solution.py
@@ -61,10 +61,13 @@
 
 
 class Gather:
-    def __init__(self, me, own, view, chunk, send_sem, recv_sem, sib_send, sib_recv):
-        self.me, self.own, self.view, self.chunk = me, own, view, chunk
+    def __init__(self, me, own, buf, chunk, send_sem, recv_sem, sib_send, sib_recv):
+        self.me, self.own, self.buf, self.chunk = me, own, buf, chunk
         self.send_sem, self.recv_sem = send_sem, recv_sem
         self.sib_send, self.sib_recv = sib_send, sib_recv
+
+    def view(self, src, rows):
+        return self.buf.at[src, rows, :]
 
     def axes(self, k):
         out = []
@@ -80,8 +83,9 @@
         rows = pl.ds(k * self.chunk, self.chunk)
         slot = k * 8 + lax.div(mask, 2)
         first = self.own.at[rows, :] if not masks else self.view(src, rows)
+        recv = recv_sem.at[0] if recv_sem is self.sib_recv else recv_sem.at[slot]
         return pltpu.make_async_remote_copy(
-            src_ref=first, dst_ref=self.view(src, rows), send_sem=send_sem.at[slot], recv_sem=recv_sem.at[slot],
+            src_ref=first, dst_ref=self.view(src, rows), send_sem=send_sem.at[0], recv_sem=recv,
             device_id=(target,), device_id_type=MESH)
 
     def hop(self, k, masks, bit):
@@ -136,42 +140,27 @@
                 return carry
             lax.fori_loop(0, 3, step, 0)
 
+    def wait_items(self, items, sem):
+        ref = self.buf.at[pl.ds(0, items)]
+        pltpu.make_async_copy(ref, ref, sem.at[0]).wait()
+
     def finish(self):
-        sibling = flip(self.me, 1)
-
-        def step(n, carry):
-            k, half = lax.div(n, 8), lax.rem(n, 8)
-            rows = pl.ds(k * self.chunk, self.chunk)
-            ref = self.view(xor(sibling, 2 * half), rows)
-            pltpu.make_async_remote_copy(
-                src_ref=ref, dst_ref=ref, send_sem=self.sib_send.at[n], recv_sem=self.sib_recv.at[n],
-                device_id=(sibling,), device_id_type=MESH).wait_recv()
-            return carry
-        lax.fori_loop(0, 24, step, 0)
+        self.wait_items(8, self.sib_recv)
 
     def drain(self):
-        def step(n, carry):
-            k, half = lax.div(n, 8), lax.rem(n, 8)
-            rows = pl.ds(k * self.chunk, self.chunk)
-            ref = self.view(xor(self.me, 2 * half), rows)
-            pltpu.make_async_remote_copy(
-                src_ref=ref, dst_ref=ref, send_sem=self.sib_send.at[n], recv_sem=self.sib_recv.at[n],
-                device_id=(flip(self.me, 1),), device_id_type=MESH).wait_send()
-
-            @pl.when(half > 0)
-            def _():
-                pltpu.make_async_remote_copy(
-                    src_ref=ref, dst_ref=ref, send_sem=self.send_sem.at[n], recv_sem=self.recv_sem.at[n],
-                    device_id=(flip(self.me, 1),), device_id_type=MESH).wait_send()
-            return carry
-        lax.fori_loop(0, 24, step, 0)
+        self.wait_items(7, self.send_sem)
+        self.wait_items(8, self.sib_send)
+
+
+def wait_bytes(ref, sem):
+    pltpu.make_async_copy(ref, ref, sem).wait()
 
 
 def kernel(qt_ref, do_ref, c_ref, rt_ref, wuk_ref, wuv_ref,
            o_ref, dq_ref, dc_ref, drt_ref, dwk_ref, dwv_ref,
-           in_q, in_do, stage_o, stage_dq, stage_v, stage_k, in_v, in_k, call, kcat, kt, v, vt, sbuf, prob, qz, dk, dv,
+           in_q, in_do, stage_o, stage_dq, stage_v, stage_k, in_v, in_k, call, kcat, kt, v, vt, sbuf, prob, qz, qn, dot, dk, dv,
            ot, dqt, delta, dct, wuk, wuv, dwk_own, dwv_own,
-           q_send, q_recv, do_send, do_recv, o_send, o_recv, dq_send, dq_recv, v_send, v_recv, k_send, k_recv, local_sem,
+           q_send, q_recv, o_send, o_recv, dq_send, dq_recv, v_send, v_recv, k_send, k_recv, local_sem,
            c_send, c_recv, cs_send, cs_recv, gk_send, gk_recv, gks_send, gks_recv, gv_send, gv_recv, gvs_send, gvs_recv):
     me = lax.axis_index("cp")
 
@@ -196,20 +185,15 @@
         load.wait()
     pl.semaphore_wait(barrier, N - 1)
 
-    def send(src, dst, n, send_sem, recv_sem):
-        return pltpu.make_async_remote_copy(
-            src_ref=src, dst_ref=dst.at[me], send_sem=send_sem.at[n], recv_sem=recv_sem.at[me],
-            device_id=(xor(me, partner(n)),), device_id_type=MESH)
-
-    def take(src, dst, other, send_sem, recv_sem):
+    def send(src, dst, n, send_sem, recv):
         pltpu.make_async_remote_copy(
-            src_ref=src, dst_ref=dst.at[other], send_sem=send_sem.at[0], recv_sem=recv_sem.at[other],
-            device_id=(flip(me, 1),), device_id_type=MESH).wait_recv()
-
-    gather_c = Gather(me, call.at[me], lambda src, rows: call.at[src, rows, :], C_CHUNK, c_send, c_recv, cs_send, cs_recv)
+            src_ref=src, dst_ref=dst.at[me], send_sem=send_sem.at[0], recv_sem=recv,
+            device_id=(xor(me, partner(n)),), device_id_type=MESH).start()
+
+    gather_c = Gather(me, call.at[me], call, C_CHUNK, c_send, c_recv, cs_send, cs_recv)
     gather_c.stage0()
     pltpu.make_async_copy(qt_ref.at[me], in_q.at[me], q_recv.at[me]).start()
-    pltpu.make_async_copy(do_ref.at[me], in_do.at[me], do_recv.at[me]).start()
+    pltpu.make_async_copy(do_ref.at[me], in_do.at[me], q_recv.at[me]).start()
     dk[...] = jnp.zeros_like(dk)
     dv[...] = jnp.zeros_like(dv)
     qz[...] = jnp.zeros_like(qz)
@@ -220,8 +204,8 @@
 
     def send_q(n, carry):
         other = xor(me, partner(n))
-        send(qt_ref.at[other], in_q, n, q_send, q_recv).start()
-        send(do_ref.at[other], in_do, n, do_send, do_recv).start()
+        send(qt_ref.at[other], in_q, n, q_send, q_recv.at[me])
+        send(do_ref.at[other], in_do, n, q_send, q_recv.at[me])
         return carry
 
     lax.fori_loop(1, N, send_q, 0)
@@ -257,8 +241,7 @@
 
     def forward(n, carry):
         i = xor(me, partner(n))
-        take(qt_ref.at[i], in_q, i, q_send, q_recv)
-        take(do_ref.at[i], in_do, i, do_send, do_recv)
+        wait_bytes(call.at[0, pl.ds(0, 160), :], q_recv.at[i])
         last = lax.div(i, 2)
         base = first_prob(i)
         qz[pl.ds(0, QK), :] = in_q[i]
@@ -291,9 +274,10 @@
 
         @pl.when(n > 0)
         def _():
-            send(stage_o.at[n], o_ref, n, o_send, o_recv).start()
+            send(stage_o.at[n], o_ref, n, o_send, o_recv.at[0])
 
         do_t = transpose(in_do[i].astype(F32))
+        dot[n] = do_t.astype(BF16)
         delta[n] = jnp.broadcast_to(jnp.sum(o_t * do_t, axis=0, keepdims=True), (8, T))
 
         def value_tile(jt, c):
@@ -306,7 +290,7 @@
         return carry
 
     lax.fori_loop(0, N, forward, 0)
-    pltpu.make_async_copy(stage_o.at[0], o_ref.at[me], o_recv.at[me]).start()
+    pltpu.make_async_copy(stage_o.at[0], o_ref.at[me], o_recv.at[0]).start()
 
     def block_rows(i):
         return pl.ds(pl.multiple_of(lax.rem(i, 2) * T, T), T)
@@ -314,11 +298,6 @@
     def grad_v(n, carry):
         i = xor(me, partner(n))
         stage_v[n] = transpose(dv[lax.div(i, 2), block_rows(i), :]).astype(BF16)
-
-        @pl.when(n > 0)
-        def _():
-            send(stage_v.at[n], in_v, n, v_send, v_recv).start()
-
         return carry
 
     def weight_grad(stage, own):
@@ -331,9 +310,9 @@
         own[pl.ds(0, L), :] = transpose(dwt)
 
     lax.fori_loop(0, N, grad_v, 0)
-    pltpu.make_async_copy(stage_v.at[0], in_v.at[me], v_recv.at[me]).start()
+    pltpu.make_async_copy(stage_v.at[0], in_v.at[me], v_recv.at[0]).start()
     weight_grad(stage_v, dwv_own)
-    gather_v = Gather(me, dwv_own, lambda src, rows: dwv_ref.at[src, rows, :], W_CHUNK, gv_send, gv_recv, gvs_send, gvs_recv)
+    gather_v = Gather(me, dwv_own, dwv_ref, W_CHUNK, gv_send, gv_recv, gvs_send, gvs_recv)
     all_rows = pl.ds(0, 3 * W_CHUNK)
     own_v = pltpu.make_async_copy(dwv_own, gather_v.view(me, all_rows), local_sem.at[5])
     own_v.start()
@@ -344,14 +323,18 @@
         last = lax.div(i, 2)
         base = first_prob(i)
         qz[pl.ds(0, QK), :] = in_q[i]
+        qn[...] = transpose(qz[...].astype(F32)).astype(BF16)
         dqt[...] = jnp.zeros_like(dqt)
         row_delta = delta[n, pl.ds(0, 1), :]
 
+        sbuf[0] = nn_dot(v[0], dot[n])
+
         def back_tile(jt, c):
-            dp = nt_dot(v[jt], in_do[i])
-            ds = (prob[base + jt].astype(F32) * (dp - row_delta)).astype(BF16)
-            dk[jt] += nt_dot(ds, qz[...])
+            ds = (prob[base + jt].astype(F32) * (sbuf[jt] - row_delta)).astype(BF16)
+            dp = nn_dot(v[lax.rem(jt + 1, NT)], dot[n])
+            dk[jt] += nn_dot(ds, qn[...])
             dqt[...] += nn_dot(kt[jt], ds)
+            sbuf[jt + 1] = dp
             return c
 
         lax.fori_loop(0, last + 1, back_tile, 0)
@@ -359,24 +342,25 @@
 
         @pl.when(n > 0)
         def _():
-            send(stage_dq.at[n], dq_ref, n, dq_send, dq_recv).start()
-
-        @pl.when(n == 4)
+            send(stage_dq.at[n], dq_ref, n, dq_send, dq_recv.at[0])
+            send(stage_v.at[n], in_v, n, v_send, v_recv.at[0])
+
+        @pl.when(n == 3)
         def _():
             gather_v.stage1()
 
-        @pl.when(n == 8)
+        @pl.when(n == 7)
         def _():
             gather_v.stage2()
 
-        @pl.when(n == 12)
+        @pl.when(n == 11)
         def _():
             gather_v.stage3()
 
         return carry
 
     lax.fori_loop(0, N, backward, 0)
-    pltpu.make_async_copy(stage_dq.at[0], dq_ref.at[me], dq_recv.at[me]).start()
+    pltpu.make_async_copy(stage_dq.at[0], dq_ref.at[me], dq_recv.at[0]).start()
 
     def grad_k(n, carry):
         i = xor(me, partner(n))
@@ -385,15 +369,15 @@
         return carry
 
     lax.fori_loop(0, N, grad_k, 0)
-    pltpu.make_async_copy(stage_k.at[0], in_k.at[me], k_recv.at[me]).start()
+    pltpu.make_async_copy(stage_k.at[0], in_k.at[me], k_recv.at[0]).start()
 
     def send_k(n, carry):
-        send(stage_k.at[n], in_k, n, k_send, k_recv).start()
+        send(stage_k.at[n], in_k, n, k_send, k_recv.at[0])
         return carry
 
     lax.fori_loop(1, 4, send_k, 0)
     weight_grad(stage_k, dwk_own)
-    gather_k = Gather(me, dwk_own, lambda src, rows: dwk_ref.at[src, rows, :], W_CHUNK, gk_send, gk_recv, gks_send, gks_recv)
+    gather_k = Gather(me, dwk_own, dwk_ref, W_CHUNK, gk_send, gk_recv, gks_send, gks_recv)
     own_k = pltpu.make_async_copy(dwk_own, gather_k.view(me, all_rows), local_sem.at[6])
     own_k.start()
     gather_k.stage0()
@@ -401,8 +385,9 @@
 
     dct[...] = jnp.zeros_like(dct)
 
+    wait_bytes(in_v, v_recv.at[0])
+
     def latent_from_v(h, carry):
-        take(stage_v.at[0], in_v, h, v_send, v_recv)
         cols = pl.ds(pl.multiple_of(h * D, D), D)
         dct[...] += nn_dot(wuv[:, cols], in_v[h])
         return carry
@@ -412,9 +397,9 @@
     lax.fori_loop(8, N, send_k, 0)
     gather_k.stage2()
 
-    def latent_from_k(n, acc):
-        h = xor(me, partner(n))
-        take(stage_k.at[0], in_k, h, k_send, k_recv)
+    wait_bytes(in_k, k_recv.at[0])
+
+    def latent_from_k(h, acc):
         cols = pl.ds(pl.multiple_of(h * D, D), D)
         dct[...] += nn_dot(wuk[:, cols], in_k[h, pl.ds(0, D), :])
         return acc + in_k[h, pl.ds(D, R), :].astype(F32)
@@ -428,24 +413,15 @@
     own_v.wait()
     own_k.wait()
 
-    def take_o(h, carry):
-        take(stage_o.at[0], o_ref, h, o_send, o_recv)
-        take(stage_dq.at[0], dq_ref, h, dq_send, dq_recv)
-        return carry
-
-    lax.fori_loop(0, N, take_o, 0)
-
-    def drain(n, carry):
-        other = xor(me, partner(n))
-        send(qt_ref.at[other], in_q, n, q_send, q_recv).wait_send()
-        send(do_ref.at[other], in_do, n, do_send, do_recv).wait_send()
-        send(stage_o.at[n], o_ref, n, o_send, o_recv).wait_send()
-        send(stage_dq.at[n], dq_ref, n, dq_send, dq_recv).wait_send()
-        send(stage_v.at[n], in_v, n, v_send, v_recv).wait_send()
-        send(stage_k.at[n], in_k, n, k_send, k_recv).wait_send()
-        return carry
-
-    lax.fori_loop(1, N, drain, 0)
+    wait_bytes(o_ref, o_recv.at[0])
+    wait_bytes(dq_ref, dq_recv.at[0])
+    others = pl.ds(0, N - 1)
+    wait_bytes(qt_ref.at[others], q_send.at[0])
+    wait_bytes(do_ref.at[others], q_send.at[0])
+    wait_bytes(stage_o.at[others], o_send.at[0])
+    wait_bytes(stage_dq.at[others], dq_send.at[0])
+    wait_bytes(stage_v.at[others], v_send.at[0])
+    wait_bytes(stage_k.at[others], k_send.at[0])
     gather_c.drain()
     gather_v.drain()
     gather_k.drain()
@@ -483,9 +459,11 @@
                 pltpu.VMEM((NT, QK, TK), BF16),
                 pltpu.VMEM((NT, TK, D), BF16),
                 pltpu.VMEM((NT, D, TK), BF16),
-                pltpu.VMEM((NT, TK, T), F32),
+                pltpu.VMEM((NT + 1, TK, T), F32),
                 pltpu.VMEM((NP, TK, T), BF16),
                 pltpu.VMEM((2 * D, T), BF16),
+                pltpu.VMEM((T, 2 * D), BF16),
+                pltpu.VMEM((N, D, T), BF16),
                 pltpu.VMEM((NT, TK, 2 * D), F32),
                 pltpu.VMEM((NT, TK, D), F32),
                 pltpu.VMEM((D, T), F32),
@@ -496,7 +474,7 @@
                 pltpu.VMEM((L, N * D), BF16),
                 pltpu.VMEM((3 * W_CHUNK, D), F32),
                 pltpu.VMEM((3 * W_CHUNK, D), F32),
-            ] + [dma((N,))] * 12 + [dma((7,))] + [dma((24,))] * 12,
+            ] + [dma((1,)), dma((N,))] + [dma((1,))] * 8 + [dma((7,))] + [dma((1,)), dma((24,)), dma((1,)), dma((1,))] * 3,
             compiler_params=pltpu.CompilerParams(
                 collective_id=0, has_side_effects=True, vmem_limit_bytes=67043328),
         )(jnp.transpose(queries, (1, 2, 0)), jnp.transpose(d_out, (1, 0, 2)), latent, jnp.transpose(key_rope, (1, 0)),

time: 211 us -> 218 us (1.033)
  Pallas kernels: 184 us -> 189 us
    pallas_call x1, Pallas kernels: 184 us -> 189 us  [local_step(): pl.pallas_call(kernel, name='mla_core', out_shape=(jax.ShapeDtypeStruct((...]
where the time goes in v4:
time: 218 us; the launch traced here: 216 us
  Pallas kernels  189 us (87%)
  local copies, waits for them, and re-layouts  26.2 us (12%)
    pallas_call x1, Pallas kernels, local_step(): pl.pallas_call(kernel, name='mla_core', out_shape=(jax.ShapeDtypeStruct((...  189 us
    unnamed x17, local copies, waits for them, and re-layouts  22.2 us

profile of v4, /device:TPU:0, one launch (start us, length us, event | category | flops | bytes accessed | tf_op | source)
XLA Modules:
  0.0 216.3 jit_solution(10232038159514570169)
XLA Ops:
  0.6 0.0 copy-start
  0.6 2.6 %copy.23 = bf16[256,16,128]{2,0,1:T(8,128)(2,1)} copy(bf16[256,16,128]{2,1,0:T(8,128)(2,1)} %param.11) | data formatting | bytes 2097152 | tf_op args[5]
  3.3 3.5 %copy.22 = bf16[64,8,16,128]{3,1,2,0:T(8,128)(2,1)} copy(bf16[64,8,16,128]{3,2,1,0:T(8,128)(2,1)} %bitcast.23) | data formatting | bytes 4194304
  6.7 0.0 copy-done
  6.7 1.9 copy.21
  8.6 189.5 %mla_core.1 = (bf16[16,256,128]{2,1,0:T(8,128)(2,1)}, bf16[16,192,256]{2,1,0:T(8,128)(2,1)}, bf16[256,512]{1,0:T(8,128)(2,1)}, bf16[64,256]{1,0:T(8,128)(2,1)}, ...) custom-call(bf16[16,192,256]{2,1,0:T(8,128)(2,1)} %bitcast.25, bf16[16,256,128]{2,1,0:T(8,128)(2,1)} %bitcast.22, ...), custom_call_target="tpu_custom_call" | custom-call | tf_op jit(solution)/shard_map/mla_core/pallas_call | solution.py:437
  198.0 2.9 %copy.13 = bf16[256,16,128]{2,1,0:T(8,128)(2,1)} copy(bf16[256,16,128]{2,0,1:T(8,128)(2,1)} %bitcast.27) | data formatting | bytes 2097152
  200.9 4.0 %slice_bitcast_fusion = (f32[512,16,128]{2,0,1:T(8,128)S(1)}, f32[512,16,128]{2,0,1:T(8,128)S(1)}) fusion(f32[16,528,128]{2,1,0:T(8,128)} %get-tuple-element.17, f32[16,528,128]{2,1,0:T(8,128)} %get-tuple-element.16), kind=kLoop, calls=%fused_computation | loop fusion | bytes 16777216 | tf_op jit(solution)/shard_map/transpose | solution.py:484
  205.0 4.4 %copy.15 = f32[512,16,128]{2,1,0:T(8,128)} copy(f32[512,16,128]{2,0,1:T(8,128)S(1)} %get-tuple-element.24) | data formatting | bytes 8388608
  209.4 0.0 copy-start.1
  209.4 0.0 copy-start.2
  209.4 0.0 copy-start.3
  209.4 4.4 %copy.14 = f32[512,16,128]{2,1,0:T(8,128)} copy(f32[512,16,128]{2,0,1:T(8,128)S(1)} %get-tuple-element.25) | data formatting | bytes 8388608
  213.8 0.0 copy-done.1
  213.9 1.1 copy.27
  215.0 0.0 copy-done.2
  215.0 0.7 copy.28
  215.7 0.0 copy-done.3
  215.7 0.6 copy.29
Async XLA Ops:
  0.6 6.1 %copy-start = (bf16[512,16,128]{2,1,0:T(8,128)(2,1)S(1)}, bf16[512,16,128]{2,1,0:T(8,128)(2,1)}, u32[]{:S(2)}) copy-start(bf16[512,16,128]{2,1,0:T(8,128)(2,1)} %param.10) | copy-start | bytes 6291460
  209.4 4.5 %copy-start.1 = (bf16[16,192,256]{2,1,0:T(8,128)(2,1)S(1)}, bf16[16,192,256]{2,1,0:T(8,128)(2,1)}, u32[]{:S(2)}) copy-start(bf16[16,192,256]{2,1,0:T(8,128)(2,1)} %get-tuple-element.13) | copy-start | bytes 4718596
  209.4 5.6 %copy-start.2 = (bf16[256,512]{1,0:T(8,128)(2,1)S(1)}, bf16[256,512]{1,0:T(8,128)(2,1)}, u32[]{:S(2)}) copy-start(bf16[256,512]{1,0:T(8,128)(2,1)} %get-tuple-element.34) | copy-start | bytes 786436
  209.4 6.3 %copy-start.3 = (bf16[64,256]{1,0:T(8,128)(2,1)S(1)}, bf16[64,256]{1,0:T(8,128)(2,1)}, u32[]{:S(2)}) copy-start(bf16[64,256]{1,0:T(8,128)(2,1)} %get-tuple-element.15) | copy-start | bytes 98308

commit v5 on v4

--- a/solution.py
+++ b/solution.py
@@ -20,7 +20,7 @@
 NT = 8
 C_CHUNK = 96
 W_CHUNK = 176
-NP = 72
+TILES = 9
 ORDER = (0, 7, 3, 4, 5, 2, 6, 1)
 TABLE = sum(chip << (3 * n) for n, chip in enumerate(ORDER))
 SCALE = 1.0 / math.sqrt(QK)
@@ -158,7 +158,7 @@
 
 def kernel(qt_ref, do_ref, c_ref, rt_ref, wuk_ref, wuv_ref,
            o_ref, dq_ref, dc_ref, drt_ref, dwk_ref, dwv_ref,
-           in_q, in_do, stage_o, stage_dq, stage_v, stage_k, in_v, in_k, call, kcat, kt, v, vt, sbuf, prob, qz, qn, dot, dk, dv,
+           in_q, in_do, stage_o, stage_dq, stage_v, stage_k, in_v, in_k, call, kcat, kt, v, vt, sbuf, prob, qz, qn, dot, own_do, dk, dv,
            ot, dqt, delta, dct, wuk, wuv, dwk_own, dwv_own,
            q_send, q_recv, o_send, o_recv, dq_send, dq_recv, v_send, v_recv, k_send, k_recv, local_sem,
            c_send, c_recv, cs_send, cs_recv, gk_send, gk_recv, gks_send, gks_recv, gv_send, gv_recv, gvs_send, gvs_recv):
@@ -235,61 +235,68 @@
 
     lax.fori_loop(0, NT, make_kv, 0)
 
-    def first_prob(i):
-        half = lax.div(i, 2)
-        return (half + lax.rem(i, 2)) * (half + 1)
-
-    def forward(n, carry):
-        i = xor(me, partner(n))
-        wait_bytes(call.at[0, pl.ds(0, 160), :], q_recv.at[i])
-        last = lax.div(i, 2)
-        base = first_prob(i)
-        qz[pl.ds(0, QK), :] = in_q[i]
-
-        def score_tile(jt, top):
-            sc = nn_dot(kcat[jt], qz[...])
-            sbuf[jt] = sc
-            return jnp.maximum(top, fold(sc, jnp.max))
-
-        top = lax.fori_loop(0, last, score_tile, jnp.full((8, T), -1e30, F32))
-        sc = nn_dot(kcat[last], qz[...])
-        ahead = lax.broadcasted_iota(jnp.int32, sc.shape, 0) - lax.broadcasted_iota(jnp.int32, sc.shape, 1)
-        sc = jnp.where(ahead <= i * T - last * TK, sc, -1e30)
-        sbuf[last] = sc
-        top = jnp.maximum(top, fold(sc, jnp.max))
-        top = jnp.max(top, axis=0, keepdims=True) * EXP_C
+    def pair(p):
+        na = 4 * lax.div(p, 2) + lax.rem(p, 2)
+        nb = 4 * lax.div(p, 2) + 3 - lax.rem(p, 2)
+        ia, ib = xor(me, partner(na)), xor(me, partner(nb))
+        split = lax.div(ia, 2) + 1
+        which = [jnp.minimum(lax.div(t, split), 1) for t in range(TILES)]
+        tile = [t - w * split for t, w in enumerate(which)]
+        return (na, nb), (ia, ib), which, tile
+
+    def pick(w, rows):
+        return jnp.where(w == 1, rows[1], rows[0])
+
+    def forward(p, carry):
+        steps, blocks, which, tile = pair(p)
+        for b, i in enumerate(blocks):
+            wait_bytes(call.at[0, pl.ds(0, 160), :], q_recv.at[i])
+            qz[b, pl.ds(0, QK), :] = in_q[i]
+            own_do[b] = in_do[i]
+
+        tops = [jnp.full((8, T), -1e30, F32)] * 2
+        for t in range(TILES):
+            w, jt = which[t], tile[t]
+            sc = nn_dot(kcat[jt], qz[w])
+            ahead = lax.broadcasted_iota(jnp.int32, sc.shape, 0) - lax.broadcasted_iota(jnp.int32, sc.shape, 1)
+            i = blocks[0] + w * (blocks[1] - blocks[0])
+            sc = jnp.where(ahead <= i * T - jt * TK, sc, -1e30)
+            sbuf[t] = sc
+            top = fold(sc, jnp.max)
+            tops = [jnp.where(w == b, jnp.maximum(tops[b], top), tops[b]) for b in range(2)]
+        tops = [jnp.max(x, axis=0, keepdims=True) * EXP_C for x in tops]
 
         ot[...] = jnp.zeros_like(ot)
-
-        def soft_tile(jt, total):
-            e = jnp.exp2(sbuf[jt] * EXP_C - top)
-            sbuf[jt] = e
-            ot[...] += nn_dot(vt[jt], e.astype(BF16))
-            return total + fold(e, jnp.sum)
-
-        total = lax.fori_loop(0, last + 1, soft_tile, jnp.zeros((8, T), F32))
-        inv = 1.0 / jnp.sum(total, axis=0, keepdims=True)
-        o_t = ot[...] * inv
-        stage_o[n] = transpose(o_t).astype(BF16)
-
-        @pl.when(n > 0)
-        def _():
-            send(stage_o.at[n], o_ref, n, o_send, o_recv.at[0])
-
-        do_t = transpose(in_do[i].astype(F32))
-        dot[n] = do_t.astype(BF16)
-        delta[n] = jnp.broadcast_to(jnp.sum(o_t * do_t, axis=0, keepdims=True), (8, T))
-
-        def value_tile(jt, c):
-            p = (sbuf[jt] * inv).astype(BF16)
-            prob[base + jt] = p
-            dv[jt] += nn_dot(p, in_do[i])
-            return c
-
-        lax.fori_loop(0, last + 1, value_tile, 0)
-        return carry
-
-    lax.fori_loop(0, N, forward, 0)
+        totals = [jnp.zeros((8, T), F32)] * 2
+        for t in range(TILES):
+            w, jt = which[t], tile[t]
+            e = jnp.exp2(sbuf[t] * EXP_C - pick(w, tops))
+            sbuf[t] = e
+            ot[w] += nn_dot(vt[jt], e.astype(BF16))
+            total = fold(e, jnp.sum)
+            totals = [jnp.where(w == b, totals[b] + total, totals[b]) for b in range(2)]
+        invs = [1.0 / jnp.sum(x, axis=0, keepdims=True) for x in totals]
+
+        for t in range(TILES):
+            w, jt = which[t], tile[t]
+            prob_t = (sbuf[t] * pick(w, invs)).astype(BF16)
+            prob[p * TILES + t] = prob_t
+            dv[jt] += nn_dot(prob_t, own_do[w])
+
+        for b, n in enumerate(steps):
+            o_t = ot[b] * invs[b]
+            stage_o[n] = transpose(o_t).astype(BF16)
+            do_t = transpose(own_do[b].astype(F32))
+            dot[p * 2 + b] = do_t.astype(BF16)
+            delta[p * 2 + b] = jnp.broadcast_to(jnp.sum(o_t * do_t, axis=0, keepdims=True), (8, T))
+
+            @pl.when(n > 0)
+            def _():
+                send(stage_o.at[n], o_ref, n, o_send, o_recv.at[0])
+
+        return carry
+
+    lax.fori_loop(0, N // 2, forward, 0)
     pltpu.make_async_copy(stage_o.at[0], o_ref.at[me], o_recv.at[0]).start()
 
     def block_rows(i):
@@ -318,48 +325,43 @@
     own_v.start()
     gather_v.stage0()
 
-    def backward(n, carry):
-        i = xor(me, partner(n))
-        last = lax.div(i, 2)
-        base = first_prob(i)
-        qz[pl.ds(0, QK), :] = in_q[i]
-        qn[...] = transpose(qz[...].astype(F32)).astype(BF16)
+    def backward(p, carry):
+        steps, blocks, which, tile = pair(p)
+        for b, i in enumerate(blocks):
+            qz[b, pl.ds(0, QK), :] = in_q[i]
+            qn[b] = transpose(qz[b].astype(F32)).astype(BF16)
         dqt[...] = jnp.zeros_like(dqt)
-        row_delta = delta[n, pl.ds(0, 1), :]
-
-        sbuf[0] = nn_dot(v[0], dot[n])
-
-        def back_tile(jt, c):
-            ds = (prob[base + jt].astype(F32) * (sbuf[jt] - row_delta)).astype(BF16)
-            dp = nn_dot(v[lax.rem(jt + 1, NT)], dot[n])
-            dk[jt] += nn_dot(ds, qn[...])
-            dqt[...] += nn_dot(kt[jt], ds)
-            sbuf[jt + 1] = dp
-            return c
-
-        lax.fori_loop(0, last + 1, back_tile, 0)
-        stage_dq[n] = (dqt[...] * SCALE).astype(BF16)
-
-        @pl.when(n > 0)
-        def _():
-            send(stage_dq.at[n], dq_ref, n, dq_send, dq_recv.at[0])
-            send(stage_v.at[n], in_v, n, v_send, v_recv.at[0])
-
-        @pl.when(n == 3)
+        deltas = [delta[p * 2 + b, pl.ds(0, 1), :] for b in range(2)]
+        for t in range(TILES):
+            w, jt = which[t], tile[t]
+            dp = nn_dot(v[jt], dot[p * 2 + w])
+            ds = (prob[p * TILES + t].astype(F32) * (dp - pick(w, deltas))).astype(BF16)
+            dk[jt] += nn_dot(ds, qn[w])
+            dqt[w] += nn_dot(kt[jt], ds)
+
+        for b, n in enumerate(steps):
+            stage_dq[n] = (dqt[b] * SCALE).astype(BF16)
+
+            @pl.when(n > 0)
+            def _():
+                send(stage_dq.at[n], dq_ref, n, dq_send, dq_recv.at[0])
+                send(stage_v.at[n], in_v, n, v_send, v_recv.at[0])
+
+        @pl.when(p == 2)
         def _():
             gather_v.stage1()
 
-        @pl.when(n == 7)
+        @pl.when(p == 4)
         def _():
             gather_v.stage2()
 
-        @pl.when(n == 11)
+        @pl.when(p == 6)
         def _():
             gather_v.stage3()
 
         return carry
 
-    lax.fori_loop(0, N, backward, 0)
+    lax.fori_loop(0, N // 2, backward, 0)
     pltpu.make_async_copy(stage_dq.at[0], dq_ref.at[me], dq_recv.at[0]).start()
 
     def grad_k(n, carry):
@@ -459,15 +461,16 @@
                 pltpu.VMEM((NT, QK, TK), BF16),
                 pltpu.VMEM((NT, TK, D), BF16),
                 pltpu.VMEM((NT, D, TK), BF16),
-                pltpu.VMEM((NT + 1, TK, T), F32),
-                pltpu.VMEM((NP, TK, T), BF16),
-                pltpu.VMEM((2 * D, T), BF16),
-                pltpu.VMEM((T, 2 * D), BF16),
+                pltpu.VMEM((TILES, TK, T), F32),
+                pltpu.VMEM((N // 2 * TILES, TK, T), BF16),
+                pltpu.VMEM((2, 2 * D, T), BF16),
+                pltpu.VMEM((2, T, 2 * D), BF16),
                 pltpu.VMEM((N, D, T), BF16),
+                pltpu.VMEM((2, T, D), BF16),
                 pltpu.VMEM((NT, TK, 2 * D), F32),
                 pltpu.VMEM((NT, TK, D), F32),
-                pltpu.VMEM((D, T), F32),
-                pltpu.VMEM((QK, T), F32),
+                pltpu.VMEM((2, D, T), F32),
+                pltpu.VMEM((2, QK, T), F32),
                 pltpu.VMEM((N, 8, T), F32),
                 pltpu.VMEM((L, T), F32),
                 pltpu.VMEM((L, N * D), BF16),

time: 218 us -> 179 us (0.82)
  Pallas kernels: 189 us -> 152 us
    pallas_call x1, Pallas kernels: 189 us -> 152 us  [local_step(): pl.pallas_call(kernel, name='mla_core', out_shape=(jax.ShapeDtypeStruct((...]
where the time goes in v5:
time: 179 us
  Pallas kernels  152 us (85%)
  local copies, waits for them, and re-layouts  26.2 us (15%)
    pallas_call x1, Pallas kernels, local_step(): pl.pallas_call(kernel, name='mla_core', out_shape=(jax.ShapeDtypeStruct((...  152 us
    unnamed x17, local copies, waits for them, and re-layouts  22.2 us
    transpose x1, local copies, waits for them, and re-layouts, local_step(): jnp.transpose(dwv[:, :L], (1, 0, 2))  4.04 us

profile of v5, /device:TPU:0, one launch (start us, length us, event | category | flops | bytes accessed | tf_op | source)
XLA Modules:
  0.0 179.2 jit_solution(15541092948846974637)
XLA Ops:
  0.6 0.0 copy-start
  0.6 2.6 %copy.23 = bf16[256,16,128]{2,0,1:T(8,128)(2,1)} copy(bf16[256,16,128]{2,1,0:T(8,128)(2,1)} %param.11) | data formatting | bytes 2097152 | tf_op args[5]
  3.3 3.5 %copy.22 = bf16[64,8,16,128]{3,1,2,0:T(8,128)(2,1)} copy(bf16[64,8,16,128]{3,2,1,0:T(8,128)(2,1)} %bitcast.23) | data formatting | bytes 4194304
  6.7 0.0 copy-done
  6.7 1.9 %copy.21 = bf16[64,8,16,128]{3,1,2,0:T(8,128)(2,1)} copy(bf16[64,8,16,128]{3,2,1,0:T(8,128)(2,1)S(1)} %bitcast.24) | data formatting | bytes 4194304
  8.6 152.3 %mla_core.1 = (bf16[16,256,128]{2,1,0:T(8,128)(2,1)}, bf16[16,192,256]{2,1,0:T(8,128)(2,1)}, bf16[256,512]{1,0:T(8,128)(2,1)}, bf16[64,256]{1,0:T(8,128)(2,1)}, ...) custom-call(bf16[16,192,256]{2,1,0:T(8,128)(2,1)} %bitcast.25, bf16[16,256,128]{2,1,0:T(8,128)(2,1)} %bitcast.22, ...), custom_call_target="tpu_custom_call" | custom-call | tf_op jit(solution)/shard_map/mla_core/pallas_call | solution.py:439
  160.9 2.9 %copy.13 = bf16[256,16,128]{2,1,0:T(8,128)(2,1)} copy(bf16[256,16,128]{2,0,1:T(8,128)(2,1)} %bitcast.27) | data formatting | bytes 2097152
  163.8 4.0 %slice_bitcast_fusion = (f32[512,16,128]{2,0,1:T(8,128)S(1)}, f32[512,16,128]{2,0,1:T(8,128)S(1)}) fusion(f32[16,528,128]{2,1,0:T(8,128)} %get-tuple-element.17, f32[16,528,128]{2,1,0:T(8,128)} %get-tuple-element.16), kind=kLoop, calls=%fused_computation | loop fusion | bytes 16777216 | tf_op jit(solution)/shard_map/transpose | solution.py:487
  167.8 4.4 %copy.15 = f32[512,16,128]{2,1,0:T(8,128)} copy(f32[512,16,128]{2,0,1:T(8,128)S(1)} %get-tuple-element.24) | data formatting | bytes 8388608
  172.2 0.0 copy-start.1
  172.3 0.0 copy-start.2
  172.3 0.0 copy-start.3
  172.3 4.4 %copy.14 = f32[512,16,128]{2,1,0:T(8,128)} copy(f32[512,16,128]{2,0,1:T(8,128)S(1)} %get-tuple-element.25) | data formatting | bytes 8388608
  176.7 0.0 copy-done.1
  176.7 1.1 copy.27
  177.8 0.0 copy-done.2
  177.8 0.7 copy.28
  178.5 0.0 copy-done.3
  178.6 0.6 copy.29
Async XLA Ops:
  0.6 6.1 %copy-start = (bf16[512,16,128]{2,1,0:T(8,128)(2,1)S(1)}, bf16[512,16,128]{2,1,0:T(8,128)(2,1)}, u32[]{:S(2)}) copy-start(bf16[512,16,128]{2,1,0:T(8,128)(2,1)} %param.10) | copy-start | bytes 6291460
  172.2 4.5 %copy-start.1 = (bf16[16,192,256]{2,1,0:T(8,128)(2,1)S(1)}, bf16[16,192,256]{2,1,0:T(8,128)(2,1)}, u32[]{:S(2)}) copy-start(bf16[16,192,256]{2,1,0:T(8,128)(2,1)} %get-tuple-element.13) | copy-start | bytes 4718596
  172.3 5.6 %copy-start.2 = (bf16[256,512]{1,0:T(8,128)(2,1)S(1)}, bf16[256,512]{1,0:T(8,128)(2,1)}, u32[]{:S(2)}) copy-start(bf16[256,512]{1,0:T(8,128)(2,1)} %get-tuple-element.34) | copy-start | bytes 786436
  172.3 6.3 %copy-start.3 = (bf16[64,256]{1,0:T(8,128)(2,1)S(1)}, bf16[64,256]{1,0:T(8,128)(2,1)}, u32[]{:S(2)}) copy-start(bf16[64,256]{1,0:T(8,128)(2,1)} %get-tuple-element.15) | copy-start | bytes 98308

commit v6 on v5

--- a/solution.py
+++ b/solution.py
@@ -61,13 +61,13 @@
 
 
 class Gather:
-    def __init__(self, me, own, buf, chunk, send_sem, recv_sem, sib_send, sib_recv):
-        self.me, self.own, self.buf, self.chunk = me, own, buf, chunk
+    def __init__(self, me, own, buf, by_row, chunk, send_sem, recv_sem, sib_send, sib_recv):
+        self.me, self.own, self.buf, self.by_row, self.chunk = me, own, buf, by_row, chunk
         self.send_sem, self.recv_sem = send_sem, recv_sem
         self.sib_send, self.sib_recv = sib_send, sib_recv
 
     def view(self, src, rows):
-        return self.buf.at[src, rows, :]
+        return self.buf.at[rows, src, 0, :] if self.by_row else self.buf.at[src, rows, :]
 
     def axes(self, k):
         out = []
@@ -141,7 +141,7 @@
             lax.fori_loop(0, 3, step, 0)
 
     def wait_items(self, items, sem):
-        ref = self.buf.at[pl.ds(0, items)]
+        ref = self.buf.at[:, pl.ds(0, items)] if self.by_row else self.buf.at[pl.ds(0, items)]
         pltpu.make_async_copy(ref, ref, sem.at[0]).wait()
 
     def finish(self):
@@ -159,14 +159,15 @@
 def kernel(qt_ref, do_ref, c_ref, rt_ref, wuk_ref, wuv_ref,
            o_ref, dq_ref, dc_ref, drt_ref, dwk_ref, dwv_ref,
            in_q, in_do, stage_o, stage_dq, stage_v, stage_k, in_v, in_k, call, kcat, kt, v, vt, sbuf, prob, qz, qn, dot, own_do, dk, dv,
-           ot, dqt, delta, dct, wuk, wuv, dwk_own, dwv_own,
+           ot, dqt, delta, dct, raw_w, raw_do, do_heads, wuk, wuv, dwk_own, dwv_own,
            q_send, q_recv, o_send, o_recv, dq_send, dq_recv, v_send, v_recv, k_send, k_recv, local_sem,
            c_send, c_recv, cs_send, cs_recv, gk_send, gk_recv, gks_send, gks_recv, gv_send, gv_recv, gvs_send, gvs_recv):
     me = lax.axis_index("cp")
 
     loads = [
-        pltpu.make_async_copy(wuk_ref, wuk, local_sem.at[0]),
-        pltpu.make_async_copy(wuv_ref, wuv, local_sem.at[1]),
+        pltpu.make_async_copy(wuk_ref, raw_w.at[0], local_sem.at[0]),
+        pltpu.make_async_copy(wuv_ref, raw_w.at[1], local_sem.at[1]),
+        pltpu.make_async_copy(do_ref, raw_do, local_sem.at[7]),
         pltpu.make_async_copy(c_ref, call.at[me, pl.ds(0, T), :], local_sem.at[2]),
         pltpu.make_async_copy(rt_ref.at[pl.ds(0, 32), :], call.at[me, pl.ds(T, 32), pl.ds(0, T)], local_sem.at[3]),
         pltpu.make_async_copy(rt_ref.at[pl.ds(32, 32), :], call.at[me, pl.ds(T, 32), pl.ds(T, T)], local_sem.at[4]),
@@ -181,7 +182,7 @@
         return carry
 
     lax.fori_loop(1, N, hello, 0)
-    for load in loads[2:]:
+    for load in loads[3:]:
         load.wait()
     pl.semaphore_wait(barrier, N - 1)
 
@@ -190,27 +191,51 @@
             src_ref=src, dst_ref=dst.at[me], send_sem=send_sem.at[0], recv_sem=recv,
             device_id=(xor(me, partner(n)),), device_id_type=MESH).start()
 
-    gather_c = Gather(me, call.at[me], call, C_CHUNK, c_send, c_recv, cs_send, cs_recv)
+    gather_c = Gather(me, call.at[me], call, False, C_CHUNK, c_send, c_recv, cs_send, cs_recv)
     gather_c.stage0()
     pltpu.make_async_copy(qt_ref.at[me], in_q.at[me], q_recv.at[me]).start()
-    pltpu.make_async_copy(do_ref.at[me], in_do.at[me], q_recv.at[me]).start()
     dk[...] = jnp.zeros_like(dk)
-    dv[...] = jnp.zeros_like(dv)
     qz[...] = jnp.zeros_like(qz)
     dwk_own[...] = jnp.zeros_like(dwk_own)
     dwv_own[...] = jnp.zeros_like(dwv_own)
+
+    def by_head(raw, put):
+        def spread(g, carry):
+            dv[g] = raw[pl.ds(pl.multiple_of(g * 32, 32), 32)].astype(F32).reshape(TK, D)
+            return carry
+
+        lax.fori_loop(0, NT, spread, 0)
+
+        def head(h, carry):
+            put(h, jnp.concatenate([dv[g, pl.ds(h, 32, stride=N), :] for g in range(NT)], axis=0).astype(BF16))
+            return carry
+
+        lax.fori_loop(0, N, head, 0)
+
+    def put_do(h, x):
+        do_heads[h] = x
+
+    loads[2].wait()
+    by_head(raw_do, put_do)
+    pltpu.make_async_copy(do_heads.at[me], in_do.at[me], q_recv.at[me]).start()
     gather_c.stage1()
     gather_c.stage2()
 
     def send_q(n, carry):
         other = xor(me, partner(n))
         send(qt_ref.at[other], in_q, n, q_send, q_recv.at[me])
-        send(do_ref.at[other], in_do, n, q_send, q_recv.at[me])
+        send(do_heads.at[other], in_do, n, q_send, q_recv.at[me])
         return carry
 
     lax.fori_loop(1, N, send_q, 0)
-    for load in loads[:2]:
+    for load, raw, out in ((loads[0], raw_w.at[0], wuk), (loads[1], raw_w.at[1], wuv)):
         load.wait()
+        for half in range(2):
+            def put_w(h, x):
+                out[pl.ds(half * T, T), pl.ds(pl.multiple_of(h * D, D), D)] = x
+
+            by_head(raw.at[pl.ds(half * T, T)], put_w)
+    dv[...] = jnp.zeros_like(dv)
     gather_c.stage3()
     gather_c.finish()
 
@@ -319,7 +344,7 @@
     lax.fori_loop(0, N, grad_v, 0)
     pltpu.make_async_copy(stage_v.at[0], in_v.at[me], v_recv.at[0]).start()
     weight_grad(stage_v, dwv_own)
-    gather_v = Gather(me, dwv_own, dwv_ref, W_CHUNK, gv_send, gv_recv, gvs_send, gvs_recv)
+    gather_v = Gather(me, dwv_own, dwv_ref, True, W_CHUNK, gv_send, gv_recv, gvs_send, gvs_recv)
     all_rows = pl.ds(0, 3 * W_CHUNK)
     own_v = pltpu.make_async_copy(dwv_own, gather_v.view(me, all_rows), local_sem.at[5])
     own_v.start()
@@ -379,7 +404,7 @@
 
     lax.fori_loop(1, 4, send_k, 0)
     weight_grad(stage_k, dwk_own)
-    gather_k = Gather(me, dwk_own, dwk_ref, W_CHUNK, gk_send, gk_recv, gks_send, gks_recv)
+    gather_k = Gather(me, dwk_own, dwk_ref, True, W_CHUNK, gk_send, gk_recv, gks_send, gks_recv)
     own_k = pltpu.make_async_copy(dwk_own, gather_k.view(me, all_rows), local_sem.at[6])
     own_k.start()
     gather_k.stage0()
@@ -419,7 +444,7 @@
     wait_bytes(dq_ref, dq_recv.at[0])
     others = pl.ds(0, N - 1)
     wait_bytes(qt_ref.at[others], q_send.at[0])
-    wait_bytes(do_ref.at[others], q_send.at[0])
+    wait_bytes(do_heads.at[others], q_send.at[0])
     wait_bytes(stage_o.at[others], o_send.at[0])
     wait_bytes(stage_dq.at[others], dq_send.at[0])
     wait_bytes(stage_v.at[others], v_send.at[0])
@@ -427,6 +452,18 @@
     gather_c.drain()
     gather_v.drain()
     gather_k.drain()
+
+
+def copy_kernel(a_ref, b_ref, c_ref, d_ref):
+    c_ref[...] = a_ref[...]
+    d_ref[...] = b_ref[...]
+
+
+def final_rows(a, b):
+    spec = pl.BlockSpec((64, N, D), lambda r: (r, 0, 0))
+    shape = jax.ShapeDtypeStruct((L, N, D), F32)
+    return pl.pallas_call(copy_kernel, name="final_rows", grid=(L // 64,), in_specs=[spec, spec], out_specs=(spec, spec),
+                          out_shape=(shape, shape))(a, b)
 
 
 def solution(mesh):
@@ -443,8 +480,8 @@
                        jax.ShapeDtypeStruct((N, QK, T), BF16),
                        jax.ShapeDtypeStruct((T, L), BF16),
                        jax.ShapeDtypeStruct((R, T), BF16),
-                       jax.ShapeDtypeStruct((N, 3 * W_CHUNK, D), F32),
-                       jax.ShapeDtypeStruct((N, 3 * W_CHUNK, D), F32)),
+                       jax.ShapeDtypeStruct((3 * W_CHUNK, N, 1, D), F32),
+                       jax.ShapeDtypeStruct((3 * W_CHUNK, N, 1, D), F32)),
             in_specs=[any_spec] * 6,
             out_specs=(any_spec, any_spec, vmem_spec, vmem_spec, any_spec, any_spec),
             scratch_shapes=[
@@ -473,18 +510,21 @@
                 pltpu.VMEM((2, QK, T), F32),
                 pltpu.VMEM((N, 8, T), F32),
                 pltpu.VMEM((L, T), F32),
+                pltpu.VMEM((2, L, N, D), BF16),
+                pltpu.VMEM((T, N, D), BF16),
+                pltpu.VMEM((N, T, D), BF16),
                 pltpu.VMEM((L, N * D), BF16),
                 pltpu.VMEM((L, N * D), BF16),
                 pltpu.VMEM((3 * W_CHUNK, D), F32),
                 pltpu.VMEM((3 * W_CHUNK, D), F32),
-            ] + [dma((1,)), dma((N,))] + [dma((1,))] * 8 + [dma((7,))] + [dma((1,)), dma((24,)), dma((1,)), dma((1,))] * 3,
+            ] + [dma((1,)), dma((N,))] + [dma((1,))] * 8 + [dma((8,))] + [dma((1,)), dma((24,)), dma((1,)), dma((1,))] * 3,
             compiler_params=pltpu.CompilerParams(
                 collective_id=0, has_side_effects=True, vmem_limit_bytes=67043328),
-        )(jnp.transpose(queries, (1, 2, 0)), jnp.transpose(d_out, (1, 0, 2)), latent, jnp.transpose(key_rope, (1, 0)),
-          w_uk.reshape(L, N * D), w_uv.reshape(L, N * D))
+        )(jnp.transpose(queries, (1, 2, 0)), d_out, latent, jnp.transpose(key_rope, (1, 0)),
+          w_uk, w_uv)
 
         return (jnp.transpose(o_all, (1, 0, 2)), jnp.transpose(dq_all, (2, 0, 1)), dc, jnp.transpose(drt, (1, 0)),
-                jnp.transpose(dwk[:, :L], (1, 0, 2)), jnp.transpose(dwv[:, :L], (1, 0, 2)))
+                *final_rows(dwk.reshape(3 * W_CHUNK, N, D), dwv.reshape(3 * W_CHUNK, N, D)))
 
     return jax.shard_map(local_step, mesh=mesh,
                          in_specs=(seq_spec, seq_spec, seq_spec, P(), P(), seq_spec),

time: 179 us -> 168 us (0.939)
  local copies, waits for them, and re-layouts: 26.2 us -> 5.35 us
  Pallas kernels: 152 us -> 162 us
    unnamed x17 -> x10, local copies, waits for them, and re-layouts: 22.2 us -> 5.35 us
    pallas_call x0 -> x1, Pallas kernels: none -> 8.97 us  [final_rows(): pl.pallas_call(copy_kernel, name='final_rows', grid=(L // 64,), in_specs=...]
    transpose x1 -> x0, local copies, waits for them, and re-layouts: 4.04 us -> none  [local_step(): jnp.transpose(dwv[:, :L], (1, 0, 2))]
where the time goes in v6:
time: 168 us
  Pallas kernels  162 us (96%)
  local copies, waits for them, and re-layouts  5.35 us (3%)
    pallas_call x1, Pallas kernels, local_step(): pl.pallas_call(kernel, name='mla_core', out_shape=(jax.ShapeDtypeStruct((...  153 us
    pallas_call x1, Pallas kernels, final_rows(): pl.pallas_call(copy_kernel, name='final_rows', grid=(L // 64,), in_specs=...  8.97 us
    unnamed x10, local copies, waits for them, and re-layouts  5.35 us

profile of v6, /device:TPU:0, one launch (start us, length us, event | category | flops | bytes accessed | tf_op | source)
XLA Modules:
  0.0 167.9 jit_solution(7277568149069900580)
XLA Ops:
  0.6 152.9 %mla_core.1 = (bf16[16,256,128]{2,1,0:T(8,128)(2,1)}, bf16[16,192,256]{2,1,0:T(8,128)(2,1)}, bf16[256,512]{1,0:T(8,128)(2,1)}, bf16[64,256]{1,0:T(8,128)(2,1)}, ...) custom-call(bf16[16,192,256]{2,1,0:T(8,128)(2,1)} %bitcast.9, bf16[256,16,128]{2,1,0:T(8,128)(2,1)} %do_ref.1, ...), custom_call_target="tpu_custom_call" | custom-call | tf_op jit(solution)/shard_map/mla_core/pallas_call | solution.py:476
  153.5 2.9 %copy.12 = bf16[256,16,128]{2,1,0:T(8,128)(2,1)} copy(bf16[256,16,128]{2,0,1:T(8,128)(2,1)} %bitcast.11) | data formatting | bytes 2097152
  156.4 0.0 copy-start
  156.4 9.0 %final_rows.1 = (f32[512,16,128]{2,1,0:T(8,128)}, f32[512,16,128]{2,1,0:T(8,128)}) custom-call(f32[528,16,128]{2,1,0:T(8,128)} %bitcast.7, f32[528,16,128]{2,1,0:T(8,128)} %bitcast.8), custom_call_target="tpu_custom_call" | custom-call | tf_op jit(solution)/shard_map/final_rows/pallas_call | solution.py:465
  165.4 0.0 copy-start.1
  165.4 0.0 copy-start.2
  165.4 0.0 copy-done
  165.4 1.1 copy.16
  166.5 0.0 copy-done.1
  166.5 0.7 copy.17
  167.2 0.0 copy-done.2
  167.2 0.6 copy.18
Async XLA Ops:
  156.4 9.0 %copy-start = (bf16[16,192,256]{2,1,0:T(8,128)(2,1)S(1)}, bf16[16,192,256]{2,1,0:T(8,128)(2,1)}, u32[]{:S(2)}) copy-start(bf16[16,192,256]{2,1,0:T(8,128)(2,1)} %get-tuple-element.15) | copy-start | bytes 4718596
  165.4 1.2 copy-start.1
  165.4 1.9 %copy-start.2 = (bf16[64,256]{1,0:T(8,128)(2,1)S(1)}, bf16[64,256]{1,0:T(8,128)(2,1)}, u32[]{:S(2)}) copy-start(bf16[64,256]{1,0:T(8,128)(2,1)} %get-tuple-element.17) | copy-start | bytes 98308

commit v7 on v6

--- a/solution.py
+++ b/solution.py
@@ -215,19 +215,26 @@
     def put_do(h, x):
         do_heads[h] = x
 
+    def send_q(n, carry):
+        send(qt_ref.at[xor(me, partner(n))], in_q, n, q_send, q_recv.at[me])
+        return carry
+
+    def send_do(n, carry):
+        send(do_heads.at[xor(me, partner(n))], in_do, n, q_send, q_recv.at[me])
+        return carry
+
+    def send_both(n, carry):
+        return send_do(n, send_q(n, carry))
+
+    lax.fori_loop(1, 4, send_q, 0)
     loads[2].wait()
     by_head(raw_do, put_do)
     pltpu.make_async_copy(do_heads.at[me], in_do.at[me], q_recv.at[me]).start()
     gather_c.stage1()
     gather_c.stage2()
 
-    def send_q(n, carry):
-        other = xor(me, partner(n))
-        send(qt_ref.at[other], in_q, n, q_send, q_recv.at[me])
-        send(do_heads.at[other], in_do, n, q_send, q_recv.at[me])
-        return carry
-
-    lax.fori_loop(1, N, send_q, 0)
+    lax.fori_loop(1, 4, send_do, 0)
+    lax.fori_loop(4, N, send_both, 0)
     for load, raw, out in ((loads[0], raw_w.at[0], wuk), (loads[1], raw_w.at[1], wuv)):
         load.wait()
         for half in range(2):
@@ -350,6 +357,12 @@
     own_v.start()
     gather_v.stage0()
 
+    def send_v(n, carry):
+        send(stage_v.at[n], in_v, n, v_send, v_recv.at[0])
+        return carry
+
+    lax.fori_loop(1, 8, send_v, 0)
+
     def backward(p, carry):
         steps, blocks, which, tile = pair(p)
         for b, i in enumerate(blocks):
@@ -370,17 +383,21 @@
             @pl.when(n > 0)
             def _():
                 send(stage_dq.at[n], dq_ref, n, dq_send, dq_recv.at[0])
-                send(stage_v.at[n], in_v, n, v_send, v_recv.at[0])
+
+        @pl.when(p < 4)
+        def _():
+            send_v(8 + 2 * p, 0)
+            send_v(9 + 2 * p, 0)
 
         @pl.when(p == 2)
         def _():
             gather_v.stage1()
 
-        @pl.when(p == 4)
+        @pl.when(p == 5)
         def _():
             gather_v.stage2()
 
-        @pl.when(p == 6)
+        @pl.when(p == 7)
         def _():
             gather_v.stage3()
 
@@ -396,10 +413,10 @@
         return carry
 
     lax.fori_loop(0, N, grad_k, 0)
-    pltpu.make_async_copy(stage_k.at[0], in_k.at[me], k_recv.at[0]).start()
+    pltpu.make_async_copy(stage_k.at[0], in_k.at[me], k_recv.at[me]).start()
 
     def send_k(n, carry):
-        send(stage_k.at[n], in_k, n, k_send, k_recv.at[0])
+        send(stage_k.at[n], in_k, n, k_send, k_recv.at[me])
         return carry
 
     lax.fori_loop(1, 4, send_k, 0)
@@ -408,34 +425,38 @@
     own_k = pltpu.make_async_copy(dwk_own, gather_k.view(me, all_rows), local_sem.at[6])
     own_k.start()
     gather_k.stage0()
-    lax.fori_loop(4, 8, send_k, 0)
-
+    lax.fori_loop(4, 6, send_k, 0)
+    wait_bytes(in_v, v_recv.at[0])
     dct[...] = jnp.zeros_like(dct)
-
-    wait_bytes(in_v, v_recv.at[0])
-
-    def latent_from_v(h, carry):
-        cols = pl.ds(pl.multiple_of(h * D, D), D)
-        dct[...] += nn_dot(wuv[:, cols], in_v[h])
-        return carry
-
-    lax.fori_loop(0, N, latent_from_v, 0)
     gather_k.stage1()
-    lax.fori_loop(8, N, send_k, 0)
+    lax.fori_loop(6, 10, send_k, 0)
+
+    def latent_from_v(g, carry):
+        cols = pl.ds(pl.multiple_of(g * 4 * D, 4 * D), 4 * D)
+        dct[...] += nn_dot(wuv[:, cols], in_v[pl.ds(4 * g, 4)].reshape(4 * D, T))
+        return carry
+
+    lax.fori_loop(0, 4, latent_from_v, 0)
     gather_k.stage2()
-
-    wait_bytes(in_k, k_recv.at[0])
-
-    def latent_from_k(h, acc):
-        cols = pl.ds(pl.multiple_of(h * D, D), D)
-        dct[...] += nn_dot(wuk[:, cols], in_k[h, pl.ds(0, D), :])
-        return acc + in_k[h, pl.ds(D, R), :].astype(F32)
-
-    drt_ref[...] = lax.fori_loop(0, N, latent_from_k, jnp.zeros((R, T), F32)).astype(BF16)
+    lax.fori_loop(10, N, send_k, 0)
+    gather_v.finish()
+    gather_k.stage3()
+
+    def latent_from_k(g, acc):
+        parts = []
+        for r in range(4):
+            h = xor(me, partner(4 * g + r))
+            wait_bytes(in_k.at[h], k_recv.at[h])
+            parts.append(h)
+        weights = jnp.concatenate([wuk[:, pl.ds(pl.multiple_of(h * D, D), D)] for h in parts], axis=1)
+        grads = jnp.concatenate([in_k[h, pl.ds(0, D), :] for h in parts], axis=0)
+        dct[...] += nn_dot(weights, grads)
+        for h in parts:
+            acc = acc + in_k[h, pl.ds(D, R), :].astype(F32)
+        return acc
+
+    drt_ref[...] = lax.fori_loop(0, 4, latent_from_k, jnp.zeros((R, T), F32)).astype(BF16)
     dc_ref[...] = transpose(dct[...]).astype(BF16)
-
-    gather_k.stage3()
-    gather_v.finish()
     gather_k.finish()
     own_v.wait()
     own_k.wait()
@@ -454,16 +475,52 @@
     gather_k.drain()
 
 
-def copy_kernel(a_ref, b_ref, c_ref, d_ref):
-    c_ref[...] = a_ref[...]
-    d_ref[...] = b_ref[...]
-
-
-def final_rows(a, b):
-    spec = pl.BlockSpec((64, N, D), lambda r: (r, 0, 0))
-    shape = jax.ShapeDtypeStruct((L, N, D), F32)
-    return pl.pallas_call(copy_kernel, name="final_rows", grid=(L // 64,), in_specs=[spec, spec], out_specs=(spec, spec),
-                          out_shape=(shape, shape))(a, b)
+def close_kernel(o_ref, dq_ref, dwk_ref, dwv_ref, o_out, dq_out, dwk_out, dwv_out,
+                 o_in, o_rows, o_back, dq_buf, dwk_buf, dwv_buf, sem_in, sem_out):
+    moves = []
+    for r in range(8):
+        for src, dst, buf in ((dwk_ref, dwk_out, dwk_buf), (dwv_ref, dwv_out, dwv_buf)):
+            moves.append((src, dst, buf, pl.ds(r * 64, 64)))
+    for r in range(4):
+        moves.append((dq_ref, dq_out, dq_buf, pl.ds(r * 4, 4)))
+    first = pltpu.make_async_copy(o_ref, o_in, sem_in.at[len(moves)])
+    first.start()
+    ins = [pltpu.make_async_copy(src.at[rows], buf.at[rows], sem_in.at[m]) for m, (src, dst, buf, rows) in enumerate(moves)]
+    outs = [pltpu.make_async_copy(buf.at[rows], dst.at[rows], sem_out.at[m]) for m, (src, dst, buf, rows) in enumerate(moves)]
+    for copy in ins:
+        copy.start()
+    first.wait()
+
+    def head(h, carry):
+        x = o_in[h].astype(F32)
+        for g in range(NT):
+            o_rows[g, pl.ds(h, 32, stride=N), :] = x[g * 32:(g + 1) * 32]
+        return carry
+
+    lax.fori_loop(0, N, head, 0)
+    for g in range(NT):
+        o_back[pl.ds(g * 32, 32)] = o_rows[g].reshape(32, N, D).astype(BF16)
+    last = pltpu.make_async_copy(o_back, o_out, sem_out.at[len(moves)])
+    last.start()
+    for copy, out in zip(ins, outs):
+        copy.wait()
+        out.start()
+    for out in outs:
+        out.wait()
+    last.wait()
+
+
+def close(o, dq, dwk, dwv):
+    any_spec = pl.BlockSpec(memory_space=pl.ANY)
+    dw = (L, N, D)
+    return pl.pallas_call(
+        close_kernel, name="close", in_specs=[any_spec] * 4, out_specs=(any_spec,) * 4,
+        out_shape=(jax.ShapeDtypeStruct((T, N, D), BF16), jax.ShapeDtypeStruct((N, QK, T), BF16),
+                   jax.ShapeDtypeStruct(dw, F32), jax.ShapeDtypeStruct(dw, F32)),
+        scratch_shapes=[pltpu.VMEM((N, T, D), BF16), pltpu.VMEM((NT, TK, D), F32), pltpu.VMEM((T, N, D), BF16),
+                        pltpu.VMEM((N, QK, T), BF16), pltpu.VMEM(dw, F32), pltpu.VMEM(dw, F32),
+                        pltpu.SemaphoreType.DMA((21,)), pltpu.SemaphoreType.DMA((21,))],
+        compiler_params=pltpu.CompilerParams(vmem_limit_bytes=60 << 20))(o, dq, dwk, dwv)
 
 
 def solution(mesh):
@@ -517,14 +574,14 @@
                 pltpu.VMEM((L, N * D), BF16),
                 pltpu.VMEM((3 * W_CHUNK, D), F32),
                 pltpu.VMEM((3 * W_CHUNK, D), F32),
-            ] + [dma((1,)), dma((N,))] + [dma((1,))] * 8 + [dma((8,))] + [dma((1,)), dma((24,)), dma((1,)), dma((1,))] * 3,
+            ] + [dma((1,)), dma((N,))] + [dma((1,))] * 7 + [dma((N,)), dma((8,))] + [dma((1,)), dma((24,)), dma((1,)), dma((1,))] * 3,
             compiler_params=pltpu.CompilerParams(
                 collective_id=0, has_side_effects=True, vmem_limit_bytes=67043328),
         )(jnp.transpose(queries, (1, 2, 0)), d_out, latent, jnp.transpose(key_rope, (1, 0)),
           w_uk, w_uv)
 
-        return (jnp.transpose(o_all, (1, 0, 2)), jnp.transpose(dq_all, (2, 0, 1)), dc, jnp.transpose(drt, (1, 0)),
-                *final_rows(dwk.reshape(3 * W_CHUNK, N, D), dwv.reshape(3 * W_CHUNK, N, D)))
+        o, dq, dwk, dwv = close(o_all, dq_all, dwk.reshape(3 * W_CHUNK, N, D), dwv.reshape(3 * W_CHUNK, N, D))
+        return o, jnp.transpose(dq, (2, 0, 1)), dc, jnp.transpose(drt, (1, 0)), dwk, dwv
 
     return jax.shard_map(local_step, mesh=mesh,
                          in_specs=(seq_spec, seq_spec, seq_spec, P(), P(), seq_spec),

time: 168 us -> 160 us (0.952)
  local copies, waits for them, and re-layouts: 5.35 us -> 1.33 us
  Pallas kernels: 162 us -> 158 us
    unnamed x10 -> x6, local copies, waits for them, and re-layouts: 5.35 us -> 1.33 us
    pallas_call x1, Pallas kernels: 153 us -> 150 us  [local_step(): pl.pallas_call(kernel, name='mla_core', out_shape=(jax.ShapeDtypeStruct((...]
    pallas_call x1, Pallas kernels: 8.97 us -> 7.28 us  [close(): pl.pallas_call(close_kernel, name='close', in_specs=[any_spec] * 4, out_s...]
where the time goes in v7:
time: 160 us
  Pallas kernels  158 us (99%)
    pallas_call x1, Pallas kernels, local_step(): pl.pallas_call(kernel, name='mla_core', out_shape=(jax.ShapeDtypeStruct((...  150 us
    pallas_call x1, Pallas kernels, close(): pl.pallas_call(close_kernel, name='close', in_specs=[any_spec] * 4, out_s...  7.28 us

profile of v7, /device:TPU:0, one launch (start us, length us, event | category | flops | bytes accessed | tf_op | source)
XLA Modules:
  0.0 159.6 jit_solution(6942163489783706729)
XLA Ops:
  0.6 150.3 %mla_core.1 = (bf16[16,256,128]{2,1,0:T(8,128)(2,1)}, bf16[16,192,256]{2,1,0:T(8,128)(2,1)}, bf16[256,512]{1,0:T(8,128)(2,1)}, bf16[64,256]{1,0:T(8,128)(2,1)}, ...) custom-call(bf16[16,192,256]{2,1,0:T(8,128)(2,1)} %bitcast.8, bf16[256,16,128]{2,1,0:T(8,128)(2,1)} %do_ref.1, ...), custom_call_target="tpu_custom_call" | custom-call | tf_op jit(solution)/shard_map/mla_core/pallas_call | solution.py:533
  150.9 0.0 copy-start
  151.0 0.0 copy-start.1
  151.0 7.3 %close.1 = (bf16[256,16,128]{2,1,0:T(8,128)(2,1)}, bf16[16,192,256]{2,1,0:T(8,128)(2,1)}, f32[512,16,128]{2,1,0:T(8,128)}, f32[512,16,128]{2,1,0:T(8,128)}) custom-call(bf16[16,256,128]{2,1,0:T(8,128)(2,1)} %get-tuple-element.16.o_ref, bf16[16,192,256]{2,1,0:T(8,128)(2,1)} %get-tuple-element.17.dq_ref, f32[528,16,128]{2,1,0:T(8,128)} %bitcast.6, ...), custom_call_target="tpu_custom_call" | custom-call | tf_op jit(solution)/shard_map/close/pallas_call | solution.py:516
  158.3 0.0 copy-done
  158.3 0.7 copy.14
  159.0 0.0 copy-done.1
  159.0 0.6 copy.15
Async XLA Ops:
  150.9 7.3 %copy-start = (bf16[256,512]{1,0:T(8,128)(2,1)S(1)}, bf16[256,512]{1,0:T(8,128)(2,1)}, u32[]{:S(2)}) copy-start(bf16[256,512]{1,0:T(8,128)(2,1)} %get-tuple-element.34) | copy-start | bytes 786436
  151.0 8.0 %copy-start.1 = (bf16[64,256]{1,0:T(8,128)(2,1)S(1)}, bf16[64,256]{1,0:T(8,128)(2,1)}, u32[]{:S(2)}) copy-start(bf16[64,256]{1,0:T(8,128)(2,1)} %get-tuple-element.23) | copy-start | bytes 98308

commit v8 on v7

--- a/solution.py
+++ b/solution.py
@@ -158,9 +158,9 @@
 
 def kernel(qt_ref, do_ref, c_ref, rt_ref, wuk_ref, wuv_ref,
            o_ref, dq_ref, dc_ref, drt_ref, dwk_ref, dwv_ref,
-           in_q, in_do, stage_o, stage_dq, stage_v, stage_k, in_v, in_k, call, kcat, kt, v, vt, sbuf, prob, qz, qn, dot, own_do, dk, dv,
+           in_q, in_do, stage_o, stage_dq, stage_v, stage_k, in_v, in_k, dr_part, dr_sib, dr_sum, in_dr, call, kcat, kt, v, vt, sbuf, prob, qz, qn, dot, own_do, dk, dv,
            ot, dqt, delta, dct, raw_w, raw_do, do_heads, wuk, wuv, dwk_own, dwv_own,
-           q_send, q_recv, o_send, o_recv, dq_send, dq_recv, v_send, v_recv, k_send, k_recv, local_sem,
+           q_send, q_recv, o_send, o_recv, dq_send, dq_recv, v_send, v_recv, k_send, k_recv, drs_send, drs_recv, dr_send, dr_recv, local_sem,
            c_send, c_recv, cs_send, cs_recv, gk_send, gk_recv, gks_send, gks_recv, gv_send, gv_recv, gvs_send, gvs_recv):
     me = lax.axis_index("cp")
 
@@ -223,18 +223,16 @@
         send(do_heads.at[xor(me, partner(n))], in_do, n, q_send, q_recv.at[me])
         return carry
 
-    def send_both(n, carry):
-        return send_do(n, send_q(n, carry))
-
-    lax.fori_loop(1, 4, send_q, 0)
+    lax.fori_loop(1, 8, send_q, 0)
     loads[2].wait()
     by_head(raw_do, put_do)
     pltpu.make_async_copy(do_heads.at[me], in_do.at[me], q_recv.at[me]).start()
     gather_c.stage1()
+    lax.fori_loop(1, 8, send_do, 0)
     gather_c.stage2()
 
-    lax.fori_loop(1, 4, send_do, 0)
-    lax.fori_loop(4, N, send_both, 0)
+    lax.fori_loop(8, N, send_q, 0)
+    lax.fori_loop(8, N, send_do, 0)
     for load, raw, out in ((loads[0], raw_w.at[0], wuk), (loads[1], raw_w.at[1], wuv)):
         load.wait()
         for half in range(2):
@@ -409,7 +407,8 @@
     def grad_k(n, carry):
         i = xor(me, partner(n))
         key = transpose(dk[lax.div(i, 2), block_rows(i), :] * SCALE)
-        stage_k[n] = key[:QK].astype(BF16)
+        stage_k[n] = key[:D].astype(BF16)
+        dr_part[lax.rem(n, 2), lax.div(n, 2)] = key[D:QK].astype(BF16)
         return carry
 
     lax.fori_loop(0, N, grad_k, 0)
@@ -419,6 +418,10 @@
         send(stage_k.at[n], in_k, n, k_send, k_recv.at[me])
         return carry
 
+    give = pltpu.make_async_remote_copy(
+        src_ref=dr_part.at[1], dst_ref=dr_sib, send_sem=drs_send.at[0], recv_sem=drs_recv.at[0],
+        device_id=(flip(me, 1),), device_id_type=MESH)
+    give.start()
     lax.fori_loop(1, 4, send_k, 0)
     weight_grad(stage_k, dwk_own)
     gather_k = Gather(me, dwk_own, dwk_ref, True, W_CHUNK, gk_send, gk_recv, gks_send, gks_recv)
@@ -426,6 +429,18 @@
     own_k.start()
     gather_k.stage0()
     lax.fori_loop(4, 6, send_k, 0)
+    give.wait_recv()
+    dr_sum[...] = (dr_part[0].astype(F32) + dr_sib[...].astype(F32)).astype(BF16)
+    chip = lax.div(me, 2)
+    pltpu.make_async_copy(dr_sum.at[0], in_dr.at[chip], dr_recv.at[0]).start()
+
+    def send_dr(k, carry):
+        pltpu.make_async_remote_copy(
+            src_ref=dr_sum.at[k], dst_ref=in_dr.at[chip], send_sem=dr_send.at[0], recv_sem=dr_recv.at[0],
+            device_id=(xor(me, partner(2 * k)),), device_id_type=MESH).start()
+        return carry
+
+    lax.fori_loop(1, N // 2, send_dr, 0)
     wait_bytes(in_v, v_recv.at[0])
     dct[...] = jnp.zeros_like(dct)
     gather_k.stage1()
@@ -442,20 +457,21 @@
     gather_v.finish()
     gather_k.stage3()
 
-    def latent_from_k(g, acc):
+    wait_bytes(in_dr, dr_recv.at[0])
+    drt_ref[...] = jnp.sum(in_dr[...].astype(F32), axis=0).astype(BF16)
+
+    def latent_from_k(g, carry):
         parts = []
         for r in range(4):
             h = xor(me, partner(4 * g + r))
             wait_bytes(in_k.at[h], k_recv.at[h])
             parts.append(h)
         weights = jnp.concatenate([wuk[:, pl.ds(pl.multiple_of(h * D, D), D)] for h in parts], axis=1)
-        grads = jnp.concatenate([in_k[h, pl.ds(0, D), :] for h in parts], axis=0)
+        grads = jnp.concatenate([in_k[h] for h in parts], axis=0)
         dct[...] += nn_dot(weights, grads)
-        for h in parts:
-            acc = acc + in_k[h, pl.ds(D, R), :].astype(F32)
-        return acc
-
-    drt_ref[...] = lax.fori_loop(0, 4, latent_from_k, jnp.zeros((R, T), F32)).astype(BF16)
+        return carry
+
+    lax.fori_loop(0, 4, latent_from_k, 0)
     dc_ref[...] = transpose(dct[...]).astype(BF16)
     gather_k.finish()
     own_v.wait()
@@ -470,19 +486,23 @@
     wait_bytes(stage_dq.at[others], dq_send.at[0])
     wait_bytes(stage_v.at[others], v_send.at[0])
     wait_bytes(stage_k.at[others], k_send.at[0])
+    give.wait_send()
+    wait_bytes(dr_sum.at[pl.ds(0, N // 2 - 1)], dr_send.at[0])
     gather_c.drain()
     gather_v.drain()
     gather_k.drain()
 
 
-def close_kernel(o_ref, dq_ref, dwk_ref, dwv_ref, o_out, dq_out, dwk_out, dwv_out,
-                 o_in, o_rows, o_back, dq_buf, dwk_buf, dwv_buf, sem_in, sem_out):
+def close_kernel(o_ref, dq_ref, dwk_ref, dwv_ref, dc_ref, dr_ref, o_out, dq_out, dwk_out, dwv_out, dc_out, dr_out,
+                 o_in, o_rows, o_back, dq_buf, dwk_buf, dwv_buf, dc_buf, dr_buf, sem_in, sem_out):
     moves = []
     for r in range(8):
         for src, dst, buf in ((dwk_ref, dwk_out, dwk_buf), (dwv_ref, dwv_out, dwv_buf)):
             moves.append((src, dst, buf, pl.ds(r * 64, 64)))
     for r in range(4):
         moves.append((dq_ref, dq_out, dq_buf, pl.ds(r * 4, 4)))
+    moves.append((dc_ref, dc_out, dc_buf, pl.ds(0, T)))
+    moves.append((dr_ref, dr_out, dr_buf, pl.ds(0, R)))
     first = pltpu.make_async_copy(o_ref, o_in, sem_in.at[len(moves)])
     first.start()
     ins = [pltpu.make_async_copy(src.at[rows], buf.at[rows], sem_in.at[m]) for m, (src, dst, buf, rows) in enumerate(moves)]
@@ -510,17 +530,19 @@
     last.wait()
 
 
-def close(o, dq, dwk, dwv):
+def close(*arrays):
     any_spec = pl.BlockSpec(memory_space=pl.ANY)
     dw = (L, N, D)
     return pl.pallas_call(
-        close_kernel, name="close", in_specs=[any_spec] * 4, out_specs=(any_spec,) * 4,
+        close_kernel, name="close", in_specs=[any_spec] * 6, out_specs=(any_spec,) * 6,
         out_shape=(jax.ShapeDtypeStruct((T, N, D), BF16), jax.ShapeDtypeStruct((N, QK, T), BF16),
-                   jax.ShapeDtypeStruct(dw, F32), jax.ShapeDtypeStruct(dw, F32)),
+                   jax.ShapeDtypeStruct(dw, F32), jax.ShapeDtypeStruct(dw, F32),
+                   jax.ShapeDtypeStruct((T, L), BF16), jax.ShapeDtypeStruct((R, T), BF16)),
         scratch_shapes=[pltpu.VMEM((N, T, D), BF16), pltpu.VMEM((NT, TK, D), F32), pltpu.VMEM((T, N, D), BF16),
                         pltpu.VMEM((N, QK, T), BF16), pltpu.VMEM(dw, F32), pltpu.VMEM(dw, F32),
-                        pltpu.SemaphoreType.DMA((21,)), pltpu.SemaphoreType.DMA((21,))],
-        compiler_params=pltpu.CompilerParams(vmem_limit_bytes=60 << 20))(o, dq, dwk, dwv)
+                        pltpu.VMEM((T, L), BF16), pltpu.VMEM((R, T), BF16),
+                        pltpu.SemaphoreType.DMA((23,)), pltpu.SemaphoreType.DMA((23,))],
+        compiler_params=pltpu.CompilerParams(vmem_limit_bytes=60 << 20))(*arrays)
 
 
 def solution(mesh):
@@ -547,9 +569,13 @@
                 pltpu.VMEM((N, T, D), BF16),
                 pltpu.VMEM((N, QK, T), BF16),
                 pltpu.VMEM((N, D, T), BF16),
-                pltpu.VMEM((N, QK, T), BF16),
                 pltpu.VMEM((N, D, T), BF16),
-                pltpu.VMEM((N, QK, T), BF16),
+                pltpu.VMEM((N, D, T), BF16),
+                pltpu.VMEM((N, D, T), BF16),
+                pltpu.VMEM((2, N // 2, R, T), BF16),
+                pltpu.VMEM((N // 2, R, T), BF16),
+                pltpu.VMEM((N // 2, R, T), BF16),
+                pltpu.VMEM((N // 2, R, T), BF16),
                 pltpu.VMEM((N, 3 * C_CHUNK, L), BF16),
                 pltpu.VMEM((NT, TK, 2 * D), BF16),
                 pltpu.VMEM((NT, QK, TK), BF16),
@@ -574,13 +600,14 @@
                 pltpu.VMEM((L, N * D), BF16),
                 pltpu.VMEM((3 * W_CHUNK, D), F32),
                 pltpu.VMEM((3 * W_CHUNK, D), F32),
-            ] + [dma((1,)), dma((N,))] + [dma((1,))] * 7 + [dma((N,)), dma((8,))] + [dma((1,)), dma((24,)), dma((1,)), dma((1,))] * 3,
+            ] + [dma((1,)), dma((N,))] + [dma((1,))] * 7 + [dma((N,))] + [dma((1,))] * 4 + [dma((8,))] + [dma((1,)), dma((24,)), dma((1,)), dma((1,))] * 3,
             compiler_params=pltpu.CompilerParams(
                 collective_id=0, has_side_effects=True, vmem_limit_bytes=67043328),
         )(jnp.transpose(queries, (1, 2, 0)), d_out, latent, jnp.transpose(key_rope, (1, 0)),
           w_uk, w_uv)
 
-        o, dq, dwk, dwv = close(o_all, dq_all, dwk.reshape(3 * W_CHUNK, N, D), dwv.reshape(3 * W_CHUNK, N, D))
+        o, dq, dwk, dwv, dc, drt = close(
+            o_all, dq_all, dwk.reshape(3 * W_CHUNK, N, D), dwv.reshape(3 * W_CHUNK, N, D), dc, drt)
         return o, jnp.transpose(dq, (2, 0, 1)), dc, jnp.transpose(drt, (1, 0)), dwk, dwv
 
     return jax.shard_map(local_step, mesh=mesh,

time: 160 us -> 160 us (level)
  no operation moved by 1% of the time
where the time goes in v8:
time: 160 us
  Pallas kernels  159 us (99%)
    pallas_call x1, Pallas kernels, local_step(): pl.pallas_call(kernel, name='mla_core', out_shape=(jax.ShapeDtypeStruct((...  152 us
    pallas_call x1, Pallas kernels, close(): pl.pallas_call(close_kernel, name='close', in_specs=[any_spec] * 6, out_s...  7.42 us

profile of v8, /device:TPU:0, one launch (start us, length us, event | category | flops | bytes accessed | tf_op | source)
XLA Modules:
  0.0 159.6 jit_solution(10798997619585360990)
XLA Ops:
  0.6 151.6 %mla_core.1 = (bf16[16,256,128]{2,1,0:T(8,128)(2,1)}, bf16[16,192,256]{2,1,0:T(8,128)(2,1)}, bf16[256,512]{1,0:T(8,128)(2,1)}, bf16[64,256]{1,0:T(8,128)(2,1)}, ...) custom-call(bf16[16,192,256]{2,1,0:T(8,128)(2,1)} %bitcast.8, bf16[256,16,128]{2,1,0:T(8,128)(2,1)} %do_ref.1, ...), custom_call_target="tpu_custom_call" | custom-call | tf_op jit(solution)/shard_map/mla_core/pallas_call | solution.py:555
  152.2 7.4 %close.1 = (bf16[256,16,128]{2,1,0:T(8,128)(2,1)}, bf16[16,192,256]{2,1,0:T(8,128)(2,1)}, f32[512,16,128]{2,1,0:T(8,128)}, f32[512,16,128]{2,1,0:T(8,128)}, bf16...) custom-call(bf16[16,256,128]{2,1,0:T(8,128)(2,1)} %get-tuple-element.18.o_ref, ...), custom_call_target="tpu_custom_call" | custom-call | tf_op jit(solution)/shard_map/close/pallas_call | solution.py:536

commit v9 on v8

--- a/solution.py
+++ b/solution.py
@@ -223,16 +223,18 @@
         send(do_heads.at[xor(me, partner(n))], in_do, n, q_send, q_recv.at[me])
         return carry
 
-    lax.fori_loop(1, 8, send_q, 0)
+    lax.fori_loop(1, 4, send_q, 0)
     loads[2].wait()
     by_head(raw_do, put_do)
     pltpu.make_async_copy(do_heads.at[me], in_do.at[me], q_recv.at[me]).start()
     gather_c.stage1()
-    lax.fori_loop(1, 8, send_do, 0)
     gather_c.stage2()
 
-    lax.fori_loop(8, N, send_q, 0)
-    lax.fori_loop(8, N, send_do, 0)
+    def send_both(n, carry):
+        return send_do(n, send_q(n, carry))
+
+    lax.fori_loop(1, 4, send_do, 0)
+    lax.fori_loop(4, N, send_both, 0)
     for load, raw, out in ((loads[0], raw_w.at[0], wuk), (loads[1], raw_w.at[1], wuv)):
         load.wait()
         for half in range(2):
@@ -271,7 +273,7 @@
         ia, ib = xor(me, partner(na)), xor(me, partner(nb))
         split = lax.div(ia, 2) + 1
         which = [jnp.minimum(lax.div(t, split), 1) for t in range(TILES)]
-        tile = [t - w * split for t, w in enumerate(which)]
+        tile = [split - 1] + [t - w * split - (1 - w) for t, w in enumerate(which) if t > 0]
         return (na, nb), (ia, ib), which, tile
 
     def pick(w, rows):
@@ -288,9 +290,9 @@
         for t in range(TILES):
             w, jt = which[t], tile[t]
             sc = nn_dot(kcat[jt], qz[w])
-            ahead = lax.broadcasted_iota(jnp.int32, sc.shape, 0) - lax.broadcasted_iota(jnp.int32, sc.shape, 1)
-            i = blocks[0] + w * (blocks[1] - blocks[0])
-            sc = jnp.where(ahead <= i * T - jt * TK, sc, -1e30)
+            if t in (0, TILES - 1):
+                ahead = lax.broadcasted_iota(jnp.int32, sc.shape, 0) - lax.broadcasted_iota(jnp.int32, sc.shape, 1)
+                sc = jnp.where(ahead <= blocks[t > 0] * T - jt * TK, sc, -1e30)
             sbuf[t] = sc
             top = fold(sc, jnp.max)
             tops = [jnp.where(w == b, jnp.maximum(tops[b], top), tops[b]) for b in range(2)]

time: 160 us -> 156 us (0.975)
  Pallas kernels: 159 us -> 155 us
    pallas_call x1, Pallas kernels: 152 us -> 147 us  [local_step(): pl.pallas_call(kernel, name='mla_core', out_shape=(jax.ShapeDtypeStruct((...]
where the time goes in v9:
time: 156 us; the launch traced here: 155 us
  Pallas kernels  155 us (99%)
    pallas_call x1, Pallas kernels, local_step(): pl.pallas_call(kernel, name='mla_core', out_shape=(jax.ShapeDtypeStruct((...  147 us
    pallas_call x1, Pallas kernels, close(): pl.pallas_call(close_kernel, name='close', in_specs=[any_spec] * 6, out_s...  7.42 us

profile of v9, /device:TPU:0, one launch (start us, length us, event | category | flops | bytes accessed | tf_op | source)
XLA Modules:
  0.0 155.4 jit_solution(3800622865479664726)
XLA Ops:
  0.6 147.4 %mla_core.1 = (bf16[16,256,128]{2,1,0:T(8,128)(2,1)}, bf16[16,192,256]{2,1,0:T(8,128)(2,1)}, bf16[256,512]{1,0:T(8,128)(2,1)}, bf16[64,256]{1,0:T(8,128)(2,1)}, ...) custom-call(bf16[16,192,256]{2,1,0:T(8,128)(2,1)} %bitcast.8, bf16[256,16,128]{2,1,0:T(8,128)(2,1)} %do_ref.1, ...), custom_call_target="tpu_custom_call" | custom-call | tf_op jit(solution)/shard_map/mla_core/pallas_call | solution.py:557
  148.0 7.4 %close.1 = (bf16[256,16,128]{2,1,0:T(8,128)(2,1)}, bf16[16,192,256]{2,1,0:T(8,128)(2,1)}, f32[512,16,128]{2,1,0:T(8,128)}, f32[512,16,128]{2,1,0:T(8,128)}, bf16...) custom-call(bf16[16,256,128]{2,1,0:T(8,128)(2,1)} %get-tuple-element.18.o_ref, ...), custom_call_target="tpu_custom_call" | custom-call | tf_op jit(solution)/shard_map/close/pallas_call | solution.py:538

commit v10 on v9

--- a/solution.py
+++ b/solution.py
@@ -389,48 +389,46 @@
             send_v(8 + 2 * p, 0)
             send_v(9 + 2 * p, 0)
 
-        @pl.when(p == 2)
+        @pl.when(p == 4)
         def _():
             gather_v.stage1()
 
-        @pl.when(p == 5)
-        def _():
-            gather_v.stage2()
-
-        @pl.when(p == 7)
-        def _():
-            gather_v.stage3()
-
         return carry
 
     lax.fori_loop(0, N // 2, backward, 0)
+    gather_v.stage2()
     pltpu.make_async_copy(stage_dq.at[0], dq_ref.at[me], dq_recv.at[0]).start()
+
+    def send_k(n, carry):
+        send(stage_k.at[n], in_k, n, k_send, k_recv.at[me])
+        return carry
 
     def grad_k(n, carry):
         i = xor(me, partner(n))
         key = transpose(dk[lax.div(i, 2), block_rows(i), :] * SCALE)
         stage_k[n] = key[:D].astype(BF16)
         dr_part[lax.rem(n, 2), lax.div(n, 2)] = key[D:QK].astype(BF16)
+
+        @pl.when(lax.rem(n, 6) > 0)
+        def _():
+            @pl.when(n < 6)
+            def _():
+                send_k(n, 0)
+
         return carry
 
     lax.fori_loop(0, N, grad_k, 0)
     pltpu.make_async_copy(stage_k.at[0], in_k.at[me], k_recv.at[me]).start()
-
-    def send_k(n, carry):
-        send(stage_k.at[n], in_k, n, k_send, k_recv.at[me])
-        return carry
 
     give = pltpu.make_async_remote_copy(
         src_ref=dr_part.at[1], dst_ref=dr_sib, send_sem=drs_send.at[0], recv_sem=drs_recv.at[0],
         device_id=(flip(me, 1),), device_id_type=MESH)
     give.start()
-    lax.fori_loop(1, 4, send_k, 0)
     weight_grad(stage_k, dwk_own)
     gather_k = Gather(me, dwk_own, dwk_ref, True, W_CHUNK, gk_send, gk_recv, gks_send, gks_recv)
     own_k = pltpu.make_async_copy(dwk_own, gather_k.view(me, all_rows), local_sem.at[6])
     own_k.start()
     gather_k.stage0()
-    lax.fori_loop(4, 6, send_k, 0)
     give.wait_recv()
     dr_sum[...] = (dr_part[0].astype(F32) + dr_sib[...].astype(F32)).astype(BF16)
     chip = lax.div(me, 2)
@@ -456,6 +454,7 @@
     lax.fori_loop(0, 4, latent_from_v, 0)
     gather_k.stage2()
     lax.fori_loop(10, N, send_k, 0)
+    gather_v.stage3()
     gather_v.finish()
     gather_k.stage3()
 

time: 156 us -> 155 us (level)
  no operation moved by 1% of the time
where the time goes in v10:
time: 155 us
  Pallas kernels  154 us (99%)
    pallas_call x1, Pallas kernels, local_step(): pl.pallas_call(kernel, name='mla_core', out_shape=(jax.ShapeDtypeStruct((...  147 us
    pallas_call x1, Pallas kernels, close(): pl.pallas_call(close_kernel, name='close', in_specs=[any_spec] * 6, out_s...  7.42 us

profile of v10, /device:TPU:0, one launch (start us, length us, event | category | flops | bytes accessed | tf_op | source)
XLA Modules:
  0.0 154.7 jit_solution(17935505438465078026)
XLA Ops:
  0.6 146.6 %mla_core.1 = (bf16[16,256,128]{2,1,0:T(8,128)(2,1)}, bf16[16,192,256]{2,1,0:T(8,128)(2,1)}, bf16[256,512]{1,0:T(8,128)(2,1)}, bf16[64,256]{1,0:T(8,128)(2,1)}, ...) custom-call(bf16[16,192,256]{2,1,0:T(8,128)(2,1)} %bitcast.8, bf16[256,16,128]{2,1,0:T(8,128)(2,1)} %do_ref.1, ...), custom_call_target="tpu_custom_call" | custom-call | tf_op jit(solution)/shard_map/mla_core/pallas_call | solution.py:556
  147.3 7.4 %close.1 = (bf16[256,16,128]{2,1,0:T(8,128)(2,1)}, bf16[16,192,256]{2,1,0:T(8,128)(2,1)}, f32[512,16,128]{2,1,0:T(8,128)}, f32[512,16,128]{2,1,0:T(8,128)}, bf16...) custom-call(bf16[16,256,128]{2,1,0:T(8,128)(2,1)} %get-tuple-element.18.o_ref, ...), custom_call_target="tpu_custom_call" | custom-call | tf_op jit(solution)/shard_map/close/pallas_call | solution.py:537

commit v11 on v10

--- a/solution.py
+++ b/solution.py
@@ -1,3 +1,4 @@
+import functools
 import math
 import jax
 import jax.numpy as jnp
@@ -159,7 +160,7 @@
 def kernel(qt_ref, do_ref, c_ref, rt_ref, wuk_ref, wuv_ref,
            o_ref, dq_ref, dc_ref, drt_ref, dwk_ref, dwv_ref,
            in_q, in_do, stage_o, stage_dq, stage_v, stage_k, in_v, in_k, dr_part, dr_sib, dr_sum, in_dr, call, kcat, kt, v, vt, sbuf, prob, qz, qn, dot, own_do, dk, dv,
-           ot, dqt, delta, dct, raw_w, raw_do, do_heads, wuk, wuv, dwk_own, dwv_own,
+           ot, dqt, delta, dct, raw_w, raw_do, do_heads, w_own, wuk, wuv, dwk_own, dwv_own,
            q_send, q_recv, o_send, o_recv, dq_send, dq_recv, v_send, v_recv, k_send, k_recv, drs_send, drs_recv, dr_send, dr_recv, local_sem,
            c_send, c_recv, cs_send, cs_recv, gk_send, gk_recv, gks_send, gks_recv, gv_send, gv_recv, gvs_send, gvs_recv):
     me = lax.axis_index("cp")
@@ -199,15 +200,21 @@
     dwk_own[...] = jnp.zeros_like(dwk_own)
     dwv_own[...] = jnp.zeros_like(dwv_own)
 
-    def by_head(raw, put):
-        def spread(g, carry):
+    def spread(raw):
+        def step(g, carry):
             dv[g] = raw[pl.ds(pl.multiple_of(g * 32, 32), 32)].astype(F32).reshape(TK, D)
             return carry
 
-        lax.fori_loop(0, NT, spread, 0)
+        lax.fori_loop(0, NT, step, 0)
+
+    def one_head(h):
+        return jnp.concatenate([dv[g, pl.ds(h, 32, stride=N), :] for g in range(NT)], axis=0).astype(BF16)
+
+    def by_head(raw, put):
+        spread(raw)
 
         def head(h, carry):
-            put(h, jnp.concatenate([dv[g, pl.ds(h, 32, stride=N), :] for g in range(NT)], axis=0).astype(BF16))
+            put(h, one_head(h))
             return carry
 
         lax.fori_loop(0, N, head, 0)
@@ -235,25 +242,29 @@
 
     lax.fori_loop(1, 4, send_do, 0)
     lax.fori_loop(4, N, send_both, 0)
-    for load, raw, out in ((loads[0], raw_w.at[0], wuk), (loads[1], raw_w.at[1], wuv)):
-        load.wait()
+    for m in range(2):
+        loads[m].wait()
+        for half in range(2):
+            rows = pl.ds(half * T, T)
+            spread(raw_w.at[m, rows])
+            w_own[rows, pl.ds(m * D, D)] = one_head(me)
+
+    def order_weights(m, out):
         for half in range(2):
             def put_w(h, x):
                 out[pl.ds(half * T, T), pl.ds(pl.multiple_of(h * D, D), D)] = x
 
-            by_head(raw.at[pl.ds(half * T, T)], put_w)
+            by_head(raw_w.at[m, pl.ds(half * T, T)], put_w)
+
     dv[...] = jnp.zeros_like(dv)
     gather_c.stage3()
     gather_c.finish()
 
-    lanes = pl.ds(pl.multiple_of(me * D, D), D)
-
     def make_kv(jt, carry):
-        wcat = jnp.concatenate([wuk[:, lanes], wuv[:, lanes]], axis=1)
         for half in range(2):
             j = jt * 2 + half
             rows = pl.ds(half * T, T)
-            kv = nn_dot(call[j, pl.ds(0, T), :], wcat)
+            kv = nn_dot(call[j, pl.ds(0, T), :], w_own[...])
             rt = jnp.concatenate([call[j, pl.ds(T, 32), pl.ds(0, T)], call[j, pl.ds(T, 32), pl.ds(T, T)]], axis=0)
             rtz = jnp.concatenate([rt.astype(F32), jnp.zeros((R, T), F32)], axis=0)
             kcat[jt, rows, pl.ds(0, D)] = kv[:, :D].astype(BF16)
@@ -286,7 +297,7 @@
             qz[b, pl.ds(0, QK), :] = in_q[i]
             own_do[b] = in_do[i]
 
-        tops = [jnp.full((8, T), -1e30, F32)] * 2
+        tile_top, tile_sum = [], []
         for t in range(TILES):
             w, jt = which[t], tile[t]
             sc = nn_dot(kcat[jt], qz[w])
@@ -294,29 +305,27 @@
                 ahead = lax.broadcasted_iota(jnp.int32, sc.shape, 0) - lax.broadcasted_iota(jnp.int32, sc.shape, 1)
                 sc = jnp.where(ahead <= blocks[t > 0] * T - jt * TK, sc, -1e30)
             sbuf[t] = sc
-            top = fold(sc, jnp.max)
-            tops = [jnp.where(w == b, jnp.maximum(tops[b], top), tops[b]) for b in range(2)]
-        tops = [jnp.max(x, axis=0, keepdims=True) * EXP_C for x in tops]
+            top = jnp.max(fold(sc, jnp.max), axis=0, keepdims=True) * EXP_C
+            e = jnp.exp2(sbuf[t] * EXP_C - top)
+            sbuf[t] = e
+            tile_top.append(top)
+            tile_sum.append(jnp.sum(fold(e, jnp.sum), axis=0, keepdims=True))
+
+        tops = [functools.reduce(jnp.maximum, [jnp.where(w == b, x, -jnp.inf) for w, x in zip(which, tile_top)])
+                for b in range(2)]
+        factors = [jnp.exp2(x - pick(w, tops)) for w, x in zip(which, tile_top)]
+        invs = [1.0 / sum(jnp.where(w == b, x * f, 0.0) for w, x, f in zip(which, tile_sum, factors)) for b in range(2)]
 
         ot[...] = jnp.zeros_like(ot)
-        totals = [jnp.zeros((8, T), F32)] * 2
         for t in range(TILES):
             w, jt = which[t], tile[t]
-            e = jnp.exp2(sbuf[t] * EXP_C - pick(w, tops))
-            sbuf[t] = e
-            ot[w] += nn_dot(vt[jt], e.astype(BF16))
-            total = fold(e, jnp.sum)
-            totals = [jnp.where(w == b, totals[b] + total, totals[b]) for b in range(2)]
-        invs = [1.0 / jnp.sum(x, axis=0, keepdims=True) for x in totals]
-
-        for t in range(TILES):
-            w, jt = which[t], tile[t]
-            prob_t = (sbuf[t] * pick(w, invs)).astype(BF16)
+            prob_t = (sbuf[t] * (factors[t] * pick(w, invs))).astype(BF16)
             prob[p * TILES + t] = prob_t
+            ot[w] += nn_dot(vt[jt], prob_t)
             dv[jt] += nn_dot(prob_t, own_do[w])
 
         for b, n in enumerate(steps):
-            o_t = ot[b] * invs[b]
+            o_t = ot[b]
             stage_o[n] = transpose(o_t).astype(BF16)
             do_t = transpose(own_do[b].astype(F32))
             dot[p * 2 + b] = do_t.astype(BF16)
@@ -441,6 +450,7 @@
         return carry
 
     lax.fori_loop(1, N // 2, send_dr, 0)
+    order_weights(1, wuv)
     wait_bytes(in_v, v_recv.at[0])
     dct[...] = jnp.zeros_like(dct)
     gather_k.stage1()
@@ -454,6 +464,7 @@
     lax.fori_loop(0, 4, latent_from_v, 0)
     gather_k.stage2()
     lax.fori_loop(10, N, send_k, 0)
+    order_weights(0, wuk)
     gather_v.stage3()
     gather_v.finish()
     gather_k.stage3()
@@ -597,6 +608,7 @@
                 pltpu.VMEM((2, L, N, D), BF16),
                 pltpu.VMEM((T, N, D), BF16),
                 pltpu.VMEM((N, T, D), BF16),
+                pltpu.VMEM((L, 2 * D), BF16),
                 pltpu.VMEM((L, N * D), BF16),
                 pltpu.VMEM((L, N * D), BF16),
                 pltpu.VMEM((3 * W_CHUNK, D), F32),

time: 155 us -> 154 us (level)
  no operation moved by 1% of the time
where the time goes in v11:
time: 154 us
  Pallas kernels  153 us (99%)
    pallas_call x1, Pallas kernels, local_step(): pl.pallas_call(kernel, name='mla_core', out_shape=(jax.ShapeDtypeStruct((...  145 us
    pallas_call x1, Pallas kernels, close(): pl.pallas_call(close_kernel, name='close', in_specs=[any_spec] * 6, out_s...  7.42 us

profile of v11, /device:TPU:0, one launch (start us, length us, event | category | flops | bytes accessed | tf_op | source)
XLA Modules:
  0.0 153.6 jit_solution(17507706349865814679)
XLA Ops:
  0.6 145.5 %mla_core.1 = (bf16[16,256,128]{2,1,0:T(8,128)(2,1)}, bf16[16,192,256]{2,1,0:T(8,128)(2,1)}, bf16[256,512]{1,0:T(8,128)(2,1)}, bf16[64,256]{1,0:T(8,128)(2,1)}, ...) custom-call(bf16[16,192,256]{2,1,0:T(8,128)(2,1)} %bitcast.8, bf16[256,16,128]{2,1,0:T(8,128)(2,1)} %do_ref.1, ...), custom_call_target="tpu_custom_call" | custom-call | tf_op jit(solution)/shard_map/mla_core/pallas_call | solution.py:567
  146.1 7.4 %close.1 = (bf16[256,16,128]{2,1,0:T(8,128)(2,1)}, bf16[16,192,256]{2,1,0:T(8,128)(2,1)}, f32[512,16,128]{2,1,0:T(8,128)}, f32[512,16,128]{2,1,0:T(8,128)}, bf16...) custom-call(bf16[16,256,128]{2,1,0:T(8,128)(2,1)} %get-tuple-element.18.o_ref, ...), custom_call_target="tpu_custom_call" | custom-call | tf_op jit(solution)/shard_map/close/pallas_call | solution.py:548

commit v12 on v11

--- a/solution.py
+++ b/solution.py
@@ -360,7 +360,7 @@
     lax.fori_loop(0, N, grad_v, 0)
     pltpu.make_async_copy(stage_v.at[0], in_v.at[me], v_recv.at[0]).start()
     weight_grad(stage_v, dwv_own)
-    gather_v = Gather(me, dwv_own, dwv_ref, True, W_CHUNK, gv_send, gv_recv, gvs_send, gvs_recv)
+    gather_v = Gather(me, dwv_own, dwv_ref, False, W_CHUNK, gv_send, gv_recv, gvs_send, gvs_recv)
     all_rows = pl.ds(0, 3 * W_CHUNK)
     own_v = pltpu.make_async_copy(dwv_own, gather_v.view(me, all_rows), local_sem.at[5])
     own_v.start()
@@ -434,7 +434,7 @@
         device_id=(flip(me, 1),), device_id_type=MESH)
     give.start()
     weight_grad(stage_k, dwk_own)
-    gather_k = Gather(me, dwk_own, dwk_ref, True, W_CHUNK, gk_send, gk_recv, gks_send, gks_recv)
+    gather_k = Gather(me, dwk_own, dwk_ref, False, W_CHUNK, gk_send, gk_recv, gks_send, gks_recv)
     own_k = pltpu.make_async_copy(dwk_own, gather_k.view(me, all_rows), local_sem.at[6])
     own_k.start()
     gather_k.stage0()
@@ -508,17 +508,17 @@
 def close_kernel(o_ref, dq_ref, dwk_ref, dwv_ref, dc_ref, dr_ref, o_out, dq_out, dwk_out, dwv_out, dc_out, dr_out,
                  o_in, o_rows, o_back, dq_buf, dwk_buf, dwv_buf, dc_buf, dr_buf, sem_in, sem_out):
     moves = []
-    for r in range(8):
+    rows = pl.ds(0, L)
+    for h in range(N):
         for src, dst, buf in ((dwk_ref, dwk_out, dwk_buf), (dwv_ref, dwv_out, dwv_buf)):
-            moves.append((src, dst, buf, pl.ds(r * 64, 64)))
-    for r in range(4):
-        moves.append((dq_ref, dq_out, dq_buf, pl.ds(r * 4, 4)))
-    moves.append((dc_ref, dc_out, dc_buf, pl.ds(0, T)))
-    moves.append((dr_ref, dr_out, dr_buf, pl.ds(0, R)))
+            moves.append((src.at[h, rows], dst.at[:, h, 0], buf.at[h]))
+    moves.append((dq_ref, dq_out, dq_buf))
+    moves.append((dc_ref, dc_out, dc_buf))
+    moves.append((dr_ref, dr_out, dr_buf))
     first = pltpu.make_async_copy(o_ref, o_in, sem_in.at[len(moves)])
     first.start()
-    ins = [pltpu.make_async_copy(src.at[rows], buf.at[rows], sem_in.at[m]) for m, (src, dst, buf, rows) in enumerate(moves)]
-    outs = [pltpu.make_async_copy(buf.at[rows], dst.at[rows], sem_out.at[m]) for m, (src, dst, buf, rows) in enumerate(moves)]
+    ins = [pltpu.make_async_copy(src, buf, sem_in.at[m]) for m, (src, dst, buf) in enumerate(moves)]
+    outs = [pltpu.make_async_copy(buf, dst, sem_out.at[m]) for m, (src, dst, buf) in enumerate(moves)]
     for copy in ins:
         copy.start()
     first.wait()
@@ -544,16 +544,17 @@
 
 def close(*arrays):
     any_spec = pl.BlockSpec(memory_space=pl.ANY)
-    dw = (L, N, D)
+    dw = (L, N, 1, D)
+    dw_buf = (N, L, D)
     return pl.pallas_call(
         close_kernel, name="close", in_specs=[any_spec] * 6, out_specs=(any_spec,) * 6,
         out_shape=(jax.ShapeDtypeStruct((T, N, D), BF16), jax.ShapeDtypeStruct((N, QK, T), BF16),
                    jax.ShapeDtypeStruct(dw, F32), jax.ShapeDtypeStruct(dw, F32),
                    jax.ShapeDtypeStruct((T, L), BF16), jax.ShapeDtypeStruct((R, T), BF16)),
         scratch_shapes=[pltpu.VMEM((N, T, D), BF16), pltpu.VMEM((NT, TK, D), F32), pltpu.VMEM((T, N, D), BF16),
-                        pltpu.VMEM((N, QK, T), BF16), pltpu.VMEM(dw, F32), pltpu.VMEM(dw, F32),
+                        pltpu.VMEM((N, QK, T), BF16), pltpu.VMEM(dw_buf, F32), pltpu.VMEM(dw_buf, F32),
                         pltpu.VMEM((T, L), BF16), pltpu.VMEM((R, T), BF16),
-                        pltpu.SemaphoreType.DMA((23,)), pltpu.SemaphoreType.DMA((23,))],
+                        pltpu.SemaphoreType.DMA((36,)), pltpu.SemaphoreType.DMA((36,))],
         compiler_params=pltpu.CompilerParams(vmem_limit_bytes=60 << 20))(*arrays)
 
 
@@ -571,8 +572,8 @@
                        jax.ShapeDtypeStruct((N, QK, T), BF16),
                        jax.ShapeDtypeStruct((T, L), BF16),
                        jax.ShapeDtypeStruct((R, T), BF16),
-                       jax.ShapeDtypeStruct((3 * W_CHUNK, N, 1, D), F32),
-                       jax.ShapeDtypeStruct((3 * W_CHUNK, N, 1, D), F32)),
+                       jax.ShapeDtypeStruct((N, 3 * W_CHUNK, D), F32),
+                       jax.ShapeDtypeStruct((N, 3 * W_CHUNK, D), F32)),
             in_specs=[any_spec] * 6,
             out_specs=(any_spec, any_spec, vmem_spec, vmem_spec, any_spec, any_spec),
             scratch_shapes=[
@@ -620,8 +621,8 @@
           w_uk, w_uv)
 
         o, dq, dwk, dwv, dc, drt = close(
-            o_all, dq_all, dwk.reshape(3 * W_CHUNK, N, D), dwv.reshape(3 * W_CHUNK, N, D), dc, drt)
-        return o, jnp.transpose(dq, (2, 0, 1)), dc, jnp.transpose(drt, (1, 0)), dwk, dwv
+            o_all, dq_all, dwk, dwv, dc, drt)
+        return o, jnp.transpose(dq, (2, 0, 1)), dc, jnp.transpose(drt, (1, 0)), dwk.reshape(L, N, D), dwv.reshape(L, N, D)
 
     return jax.shard_map(local_step, mesh=mesh,
                          in_specs=(seq_spec, seq_spec, seq_spec, P(), P(), seq_spec),

time: 154 us -> 154 us (level)
  no operation moved by 1% of the time
where the time goes in v12:
time: 154 us
  Pallas kernels  153 us (99%)
    pallas_call x1, Pallas kernels, local_step(): pl.pallas_call(kernel, name='mla_core', out_shape=(jax.ShapeDtypeStruct((...  145 us
    pallas_call x1, Pallas kernels, close(): pl.pallas_call(close_kernel, name='close', in_specs=[any_spec] * 6, out_s...  7.95 us

profile of v12, /device:TPU:0, one launch (start us, length us, event | category | flops | bytes accessed | tf_op | source)
XLA Modules:
  0.0 154.1 jit_solution(5328071632323573109)
XLA Ops:
  0.6 145.5 %mla_core.1 = (bf16[16,256,128]{2,1,0:T(8,128)(2,1)}, bf16[16,192,256]{2,1,0:T(8,128)(2,1)}, bf16[256,512]{1,0:T(8,128)(2,1)}, bf16[64,256]{1,0:T(8,128)(2,1)}, ...) custom-call(bf16[16,192,256]{2,1,0:T(8,128)(2,1)} %bitcast.6, bf16[256,16,128]{2,1,0:T(8,128)(2,1)} %do_ref.1, ...), custom_call_target="tpu_custom_call" | custom-call | tf_op jit(solution)/shard_map/mla_core/pallas_call | solution.py:568
  146.1 8.0 %close.1 = (bf16[256,16,128]{2,1,0:T(8,128)(2,1)}, bf16[16,192,256]{2,1,0:T(8,128)(2,1)}, f32[512,16,1,128]{3,2,1,0:T(1,128)}, f32[512,16,1,128]{3,2,1,0:T(1,128...) custom-call(bf16[16,256,128]{2,1,0:T(8,128)(2,1)} %get-tuple-element.18.o_ref, ...), custom_call_target="tpu_custom_call" | custom-call | tf_op jit(solution)/shard_map/close/pallas_call | solution.py:549

commit v13 on v11

--- a/solution.py
+++ b/solution.py
@@ -159,11 +159,12 @@
 
 def kernel(qt_ref, do_ref, c_ref, rt_ref, wuk_ref, wuv_ref,
            o_ref, dq_ref, dc_ref, drt_ref, dwk_ref, dwv_ref,
-           in_q, in_do, stage_o, stage_dq, stage_v, stage_k, in_v, in_k, dr_part, dr_sib, dr_sum, in_dr, call, kcat, kt, v, vt, sbuf, prob, qz, qn, dot, own_do, dk, dv,
-           ot, dqt, delta, dct, raw_w, raw_do, do_heads, w_own, wuk, wuv, dwk_own, dwv_own,
+           in_q, in_do, stage_o, stage_dq, stage_v, in_v, in_k, dr_part, dr_sib, dr_sum, in_dr, call, kcat, kt, v, vt, sbuf, prob, qz, qn, dot, own_do, dk, dv,
+           ot, dqt, delta, raw_w, raw_do, do_heads, w_own, wuk, wuv, dwk_own, dwv_own,
            q_send, q_recv, o_send, o_recv, dq_send, dq_recv, v_send, v_recv, k_send, k_recv, drs_send, drs_recv, dr_send, dr_recv, local_sem,
            c_send, c_recv, cs_send, cs_recv, gk_send, gk_recv, gks_send, gks_recv, gv_send, gv_recv, gvs_send, gvs_recv):
     me = lax.axis_index("cp")
+    stage_k, dct = dot, sbuf.at[0]
 
     loads = [
         pltpu.make_async_copy(wuk_ref, raw_w.at[0], local_sem.at[0]),
@@ -276,7 +277,10 @@
             vt[jt, :, rows] = kvt[D:]
         return carry
 
-    lax.fori_loop(0, NT, make_kv, 0)
+    def make_kv_two(jt, carry):
+        return make_kv(2 * jt + 1, make_kv(2 * jt, carry))
+
+    lax.fori_loop(0, NT // 2, make_kv_two, 0)
 
     def pair(p):
         na = 4 * lax.div(p, 2) + lax.rem(p, 2)
@@ -337,7 +341,10 @@
 
         return carry
 
-    lax.fori_loop(0, N // 2, forward, 0)
+    def forward_two(p, carry):
+        return forward(2 * p + 1, forward(2 * p, carry))
+
+    lax.fori_loop(0, N // 4, forward_two, 0)
     pltpu.make_async_copy(stage_o.at[0], o_ref.at[me], o_recv.at[0]).start()
 
     def block_rows(i):
@@ -583,7 +590,6 @@
                 pltpu.VMEM((N, D, T), BF16),
                 pltpu.VMEM((N, D, T), BF16),
                 pltpu.VMEM((N, D, T), BF16),
-                pltpu.VMEM((N, D, T), BF16),
                 pltpu.VMEM((2, N // 2, R, T), BF16),
                 pltpu.VMEM((N // 2, R, T), BF16),
                 pltpu.VMEM((N // 2, R, T), BF16),
@@ -604,7 +610,6 @@
                 pltpu.VMEM((2, D, T), F32),
                 pltpu.VMEM((2, QK, T), F32),
                 pltpu.VMEM((N, 8, T), F32),
-                pltpu.VMEM((L, T), F32),
                 pltpu.VMEM((2, L, N, D), BF16),
                 pltpu.VMEM((T, N, D), BF16),
                 pltpu.VMEM((N, T, D), BF16),

time: 154 us -> 151 us (0.981)
  Pallas kernels: 153 us -> 150 us
    pallas_call x1, Pallas kernels: 145 us -> 143 us  [local_step(): pl.pallas_call(kernel, name='mla_core', out_shape=(jax.ShapeDtypeStruct((...]
where the time goes in v13:
time: 151 us
  Pallas kernels  150 us (99%)
    pallas_call x1, Pallas kernels, local_step(): pl.pallas_call(kernel, name='mla_core', out_shape=(jax.ShapeDtypeStruct((...  143 us
    pallas_call x1, Pallas kernels, close(): pl.pallas_call(close_kernel, name='close', in_specs=[any_spec] * 6, out_s...  7.42 us

profile of v13, /device:TPU:0, one launch (start us, length us, event | category | flops | bytes accessed | tf_op | source)
XLA Modules:
  0.0 150.7 jit_solution(13927953744420633130)
XLA Ops:
  0.6 142.7 %mla_core.1 = (bf16[16,256,128]{2,1,0:T(8,128)(2,1)}, bf16[16,192,256]{2,1,0:T(8,128)(2,1)}, bf16[256,512]{1,0:T(8,128)(2,1)}, bf16[64,256]{1,0:T(8,128)(2,1)}, ...) custom-call(bf16[16,192,256]{2,1,0:T(8,128)(2,1)} %bitcast.8, bf16[256,16,128]{2,1,0:T(8,128)(2,1)} %do_ref.1, ...), custom_call_target="tpu_custom_call" | custom-call | tf_op jit(solution)/shard_map/mla_core/pallas_call | solution.py:574
  143.3 7.4 %close.1 = (bf16[256,16,128]{2,1,0:T(8,128)(2,1)}, bf16[16,192,256]{2,1,0:T(8,128)(2,1)}, f32[512,16,128]{2,1,0:T(8,128)}, f32[512,16,128]{2,1,0:T(8,128)}, bf16...) custom-call(bf16[16,256,128]{2,1,0:T(8,128)(2,1)} %get-tuple-element.18.o_ref, ...), custom_call_target="tpu_custom_call" | custom-call | tf_op jit(solution)/shard_map/close/pallas_call | solution.py:555
